TPU v7x, 256 devices: a whole 4x4x8 slice. The times are simulated.
256 devices in a mesh: row: 32 (over y_hi, z, core), col: 8 (over x, y_lo).
Axes of the slice: x: 4, y: 4 (y_hi: 2, y_lo: 2; y = y_hi * 2 + y_lo), z: 8, core: 2. Of those that a mesh axis runs over, the one named last changes fastest.
Arguments:
- hidden: bfloat16 [32768, 768], P(('row', 'col')), may hold values from -6 to 6
- projection: bfloat16 [768, 512], replicated, may hold values from -0.21875 to 0.21875
- alpha: bfloat16 [32768], P(('row', 'col')), may hold values from -6 to 6
- probe_pairs: bfloat16 [32768, 32], P(('row', 'col')), may hold values from -6 to 6
- amplitude: float32 [1], replicated, may hold values from 0.5 to 2
- length_sq: float32 [1], replicated, may hold values from 512 to 1024
Outputs:
- grad_hidden: bfloat16 [32768, 768], P(('row', 'col'))
- grad_proj: float32 [768, 512], P('row')
All inputs are finite; a program needn't handle non-finite values.
Results may differ from a plain program's by a relative error of at most 0.023.
Values may be sent and summed in bfloat16 or wider, within the bound.
A program may use at most 64 MiB of HBM per device.

v0:
```python
import math

import jax
import jax.numpy as jnp
from jax import lax
from jax.sharding import PartitionSpec as P


def side_by_side(arrays, axis, dim, along):
    widths = [a.shape[along] for a in arrays]
    both = jnp.concatenate(arrays, axis=along)
    out = lax.all_gather(both, axis, axis=dim, tiled=True)
    return tuple(jnp.split(out, [sum(widths[:k]) for k in range(1, len(widths))], axis=along))


def in_blocks(x, dim, size):
    before, after = (x.shape[:dim], x.shape[dim + 1 :])
    return jnp.moveaxis(x.reshape(*before, size, -1, *after), dim, 0)


def sent_and_summed(x, axis, dim):
    blocks = in_blocks(x, dim, lax.axis_size(axis))
    arrived = lax.all_to_all(blocks, axis, split_axis=0, concat_axis=0, tiled=True)
    return arrived.astype(jnp.float32).sum(axis=0)


def sent_to_all(x, axis):
    size = lax.axis_size(axis)
    return lax.all_to_all(jnp.broadcast_to(x[None], (size, *x.shape)), axis, 0, 0, tiled=True)


def of_everyone(x, axis):
    everything = sent_to_all(x, axis)
    return jnp.sum(everything.astype(jnp.float32), axis=0)


def right_of(factors, probes):
    scale = 1.0 / (4 * probes)
    return jnp.concatenate(
        [
            factors[:, :1] * 0.5,
            factors[:, 1 + probes :] * -scale,
            factors[:, 1 : 1 + probes] * -scale,
        ],
        axis=1,
    )


def squares(feats):
    feat_f = feats.astype(jnp.float32)
    return jnp.sum(feat_f * feat_f, axis=1)


def per_device(hidden, projection, alpha, probe_pairs, amplitude, length_sq):
    feats = jnp.dot(hidden, projection, preferred_element_type=jnp.float32).astype(jnp.bfloat16)
    factors = jnp.concatenate([alpha[:, None], probe_pairs], axis=1)
    probes = probe_pairs.shape[1] // 2
    amp = amplitude[0]
    lsq = length_sq[0]
    width = feats.shape[1]

    def make_fold(rows_feat, rows_fac):
        rows_sq = squares(rows_feat)

        def fold(carry, pieces, start):
            cols_feat, cols_fac = pieces
            count = cols_feat.shape[0]
            size = math.gcd(count, 256)
            steps_feat = cols_feat.reshape(count // size, size, width)
            steps_fac = cols_fac.reshape(count // size, size, cols_fac.shape[1])

            def inner_step(state, blocks):
                block_feat, block_fac = blocks
                moved, rowsum = state
                block_sq = squares(block_feat)
                inner = jnp.dot(rows_feat, block_feat.T, preferred_element_type=jnp.float32)
                dist = rows_sq[:, None] + block_sq[None, :] - 2.0 * inner
                kern = amp * jnp.exp(-0.5 * dist / lsq)
                gmat = jnp.dot(
                    rows_fac, right_of(block_fac, probes).T, preferred_element_type=jnp.float32
                )
                weight = gmat * kern
                rowsum = rowsum + jnp.sum(weight, axis=1)
                moved = moved + jnp.dot(
                    weight.astype(jnp.bfloat16), block_feat, preferred_element_type=jnp.float32
                )
                return ((moved, rowsum), None)

            result, unused = lax.scan(inner_step, carry, (steps_feat, steps_fac))
            return result

        start_carry = (
            jnp.zeros((rows_feat.shape[0], width), jnp.float32),
            jnp.zeros((rows_feat.shape[0],), jnp.float32),
        )
        return (fold, start_carry)

    rows_feat, rows_fac = side_by_side((feats, factors), "col", 0, 1)
    fold, start_carry = make_fold(rows_feat, rows_fac)
    moved, rowsum = fold(
        start_carry,
        (
            lax.all_gather(feats, "row", axis=0, tiled=True),
            lax.all_gather(factors, "row", axis=0, tiled=True),
        ),
        jnp.int32(0),
    )
    moved_own, rowsum_own = (
        lax.psum_scatter(moved, "col", scatter_dimension=0, tiled=True),
        lax.psum_scatter(rowsum, "col", scatter_dimension=0, tiled=True),
    )
    grad_feat = (2.0 / lsq * (moved_own - rowsum_own[:, None] * feats.astype(jnp.float32))).astype(
        jnp.bfloat16
    )
    grad_hidden = jnp.dot(grad_feat, projection.T, preferred_element_type=jnp.float32).astype(
        jnp.bfloat16
    )
    partial_proj = lax.dot_general(
        hidden, grad_feat, (((0,), (0,)), ((), ())), preferred_element_type=jnp.float32
    )
    share = sent_and_summed(partial_proj.astype(jnp.bfloat16), "row", 0)
    grad_proj = of_everyone(share.astype(jnp.bfloat16), "col").astype(jnp.float32)
    return (grad_hidden, grad_proj)


def solution(mesh):
    placed = (P(("row", "col"), None), P(), P(("row", "col")), P(("row", "col"), None), P(), P())
    return jax.shard_map(
        per_device,
        mesh=mesh,
        in_specs=placed,
        out_specs=(P(("row", "col"), None), P("row", None)),
        check_vma=False,
    )
```

profile of v0, /device:TPU:1, one launch (start us, length us, event | category | flops | bytes accessed | tf_op | source)
XLA Modules:
  0.0 351.5 jit_solution(16949946160411979620)
XLA Ops:
  12.4 47.6 %all_gather.9 = bf16[4096,33]{0,1:T(8,128)(2,1)S(1)} all-gather(bf16[128,33]{0,1:T(8,128)(2,1)S(1)} %pad_maximum_fusion.1), channel_id=1, replica_groups=mesh['row'=32,'col'=8] {'row'}, dimensions={0}, use_global_device_ids=true | all-gather | bytes 278784 | tf_op jit(solution)/shard_map/all_gather | solution.py:104
  62.9 84.4 %all-gather.5.cloned.1.call-done = bf16[4096,512]{1,0:T(8,128)(2,1)} async-done(((bf16[128,512]{1,0:T(8,128)(2,1)}), bf16[4096,512]{1,0:T(8,128)(2,1)}) %all-gather.5.cloned.1.call-update) | async-done | bytes 4194320 | tf_op jit(solution)/shard_map/all_gather | solution.py:103
  147.4 100.2 %while.13 = (s32[]{:T(128)}, f32[1024,512]{1,0:T(8,128)S(1)}, f32[1024]{0:T(1024)S(1)}, bf16[16,256,33]{1,2,0:T(8,128)(2,1)S(1)}, bf16[1024,33]{1,0:T(8,128)(2,1...) while((s32[]{:T(128)}, f32[1024,512]{1,0:T(8,128)S(1)}, ...), condition=%wide.region_4.5_spmd.clone, body=%wide.region_1.4_spmd.clone.sunk | while | flops 558033408 | bytes 9350808 | solution.py:89
  148.5 3.1 fusion.43
  154.8 3.1 fusion.43
  161.1 3.1 fusion.43
  167.3 3.1 fusion.43
  173.6 3.1 fusion.43
  179.9 3.1 fusion.43
  186.1 3.1 fusion.43
  192.4 3.1 fusion.43
  198.6 3.1 fusion.43
  204.9 3.1 fusion.43
  211.2 3.1 fusion.43
  217.4 3.1 fusion.43
  223.7 3.1 fusion.43
  230.0 3.1 fusion.43
  236.2 3.1 fusion.43
  242.5 3.1 fusion.43
  250.9 15.1 %all-reduce = f32[1024]{0:T(1024)S(1)} all-reduce(f32[1024]{0:T(1024)S(1)} %get-tuple-element.56), channel_id=3, replica_groups=mesh['row'=32,'col'=8] {'col'}, use_global_device_ids=true, to_apply=%region_6.7.clone | all-reduce | flops 1024 | bytes 8192
  266.1 32.7 %reduce-scatter.2.cloned.1.call-done = f32[128,512]{1,0:T(8,128)} async-done(((f32[1024,512]{1,0:T(8,128)}), f32[128,512]{1,0:T(8,128)}) %reduce-scatter.2.cloned.1.call-update) | async-done | bytes 262160 | tf_op jit(solution)/shard_map/reduce_scatter | solution.py:109
  300.6 33.2 %all_to_all.10 = bf16[32,24,512]{2,1,0:T(8,128)(2,1)S(1)} all-to-all(bf16[32,24,512]{2,1,0:T(8,128)(2,1)S(1)} %bitcast.64), channel_id=1, replica_groups=mesh['row'=32,'col'=8] {'row'}, dimensions={0} | all-to-all | bytes 1572864 | tf_op jit(solution)/shard_map/all_to_all | solution.py:23
  334.6 4.1 %all-to-all-start.1 = ((bf16[8,24,512]{2,1,0:T(8,128)(2,1)}), bf16[8,24,512]{2,1,0:T(8,128)(2,1)S(1)}, u32[]{:S(2)}, u32[]{:S(2)}) async-start(bf16[8,24,512]{2,1,0:T(8,128)(2,1)} %broadcast_in_dim.21), calls=%async_computation.2 | async-start | bytes 393216 | tf_op jit(solution)/shard_map/all_to_all | solution.py:29
  339.8 4.5 %all-to-all-done.1 = bf16[8,24,512]{2,1,0:T(8,128)(2,1)S(1)} async-done(((bf16[8,24,512]{2,1,0:T(8,128)(2,1)}), bf16[8,24,512]{2,1,0:T(8,128)(2,1)S(1)}, u32[]{:S(2)}, u32[]{:S(2)}) %all-to-all-start.1) | async-done | bytes 196640 | tf_op jit(solution)/shard_map/all_to_all | solution.py:29
  (156 shorter events, 63.0 us)
Async XLA Ops:
  7.2 1.7 copy-start
  7.2 53.0 %all-gather.3.cloned.1.call-start = ((), (), s32[]{:S(2)}) async-start(), calls=%async_computation.3 | async-start | bytes 1474560 | tf_op jit(solution)/shard_map/all_gather | solution.py:12
  10.1 0.8 copy-start.3
  10.9 136.5 %all-gather.5.cloned.1.call-start = ((), (), s32[]{:S(2)}) async-start(), calls=%async_computation.4 | async-start | bytes 4325376 | tf_op jit(solution)/shard_map/all_gather | solution.py:103
  11.6 287.2 %reduce-scatter.2.cloned.1.call-start = ((), (), s32[]{:S(2)}) async-start(), calls=%async_computation.5 | async-start | bytes 2359296 | tf_op jit(solution)/shard_map/reduce_scatter | solution.py:109
  60.2 2.4 copy-start.2
  60.2 87.2 %slice-start = ((bf16[1024,545]{1,0:T(8,128)(2,1)}), bf16[1024,33]{1,0:T(8,128)(2,1)S(1)}, s32[]{:S(2)}) async-start(bf16[1024,545]{1,0:T(8,128)(2,1)} %all-gather.3.cloned.1.call-done), calls=%async_computation.6 | async-start | bytes 524288 | tf_op jit(solution)/shard_map/split | solution.py:13
  247.6 1.3 copy-start.1
  247.6 2.0 copy-start.6
  247.7 51.2 %copy-start.4 = (bf16[128,512]{1,0:T(8,128)(2,1)S(1)}, bf16[128,512]{1,0:T(8,128)(2,1)}, u32[]{:S(2)}) copy-start(bf16[128,512]{1,0:T(8,128)(2,1)} %copy-done.3) | copy-start | bytes 393220
  247.7 52.2 %copy-start.5 = (bf16[128,768]{1,0:T(8,128)(2,1)S(1)}, bf16[128,768]{1,0:T(8,128)(2,1)}, u32[]{:S(2)}) copy-start(bf16[128,768]{1,0:T(8,128)(2,1)} %param.8) | copy-start | bytes 589828
  334.6 9.7 %all-to-all-start.1 = ((bf16[8,24,512]{2,1,0:T(8,128)(2,1)}), bf16[8,24,512]{2,1,0:T(8,128)(2,1)S(1)}, u32[]{:S(2)}, u32[]{:S(2)}) async-start(bf16[8,24,512]{2,1,0:T(8,128)(2,1)} %broadcast_in_dim.21), calls=%async_computation.2 | async-start | bytes 393216 | tf_op jit(solution)/shard_map/all_to_all | solution.py:29
Sparse Core Ops, SparseCore 0:
  11.0 43.9 all-gather.2
  57.8 89.5 all-gather.4
  249.1 49.6 reduce-scatter.1
where the time goes:
time: 356 us; the launch traced here: 351 us
  waiting for transfers between devices  122 us (34%)
  blocking collectives  95.9 us (27%)
  matrix products  83.9 us (24%)
  other arithmetic  21.2 us (6%)
  between operations  15.3 us (4%)
  local copies, waits for them, and re-layouts  7.39 us (2%)
  starting transfers between devices  4.26 us (1%)
    all_gather x1, waiting for transfers between devices, per_device(): lax.all_gather(feats, 'row', axis=0, tiled=True)  84.4 us
    dot_general x16, matrix products, inner_step(): inner = jnp.dot(rows_feat, block_feat.T, preferred_element_type=jnp.float32)  50.4 us
    all_gather x1, blocking collectives, per_device(): lax.all_gather(factors, 'row', axis=0, tiled=True)  47.6 us
    all_to_all x1, blocking collectives, sent_and_summed(): lax.all_to_all(blocks, axis, split_axis=0, concat_axis=0, tiled=True)  33.2 us
    reduce_scatter x1, waiting for transfers between devices, per_device(): lax.psum_scatter(moved, 'col', scatter_dimension=0, tiled=True)  32.7 us
    dot_general x16, matrix products, inner_step(): jnp.dot(weight.astype(jnp.bfloat16), block_feat, preferred_element_type=j...  25.4 us
    reduce_sum x17, other arithmetic, squares(): return jnp.sum(feat_f * feat_f, axis=1)  17.6 us
    unnamed x1, blocking collectives  15.1 us
  transfers between devices with their start and end apart: 4, of which 3 were waited for; matrix products, arithmetic and copies ran while one was open for 2% of the time, Pallas kernels for 0%

commit v1 on v0

v1 whole, which is shorter than its diff:
```python
import functools
import math

import jax
import jax.numpy as jnp
from jax import lax
from jax.experimental import pallas as pl
from jax.experimental.pallas import tpu as pltpu
from jax.sharding import PartitionSpec as P

MESH = pl.DeviceIdType.MESH
NT = (((1,), (1,)), ((), ()))
TN = (((0,), (0,)), ((), ()))
BF, F32 = jnp.bfloat16, jnp.float32

NX, NY, NZ = 4, 4, 8
AUX = 128
POS = {0: 0, 4: 1, 3: 2, 5: 3, 2: 4, 6: 5, 1: 6, 7: 7}
CHUNK = 2048


def iota(shape, dim):
    return lax.broadcasted_iota(jnp.int32, shape, dim)


def aux_block(feats, alpha_row, probe, probes):
    points = feats.shape[0]
    src, lane = iota((2 * probes, AUX), 0), iota((2 * probes, AUX), 1)
    scale = 1.0 / (4 * probes)
    swapped = jnp.where(src < probes, src + probes, src - probes)
    pick = jnp.where(lane == src, 1.0, 0.0) + jnp.where(lane - 64 == swapped, -scale, 0.0)
    aux = jnp.dot(probe, pick.astype(BF), preferred_element_type=F32)
    spread = jnp.broadcast_to(alpha_row.astype(F32), (points, points))
    diag = jnp.where(iota((points, points), 0) == iota((points, points), 1), spread, 0.0)
    lane = iota((points, AUX), 1)
    put = jnp.where(lane == 2 * probes, 1.0, 0.0) + jnp.where(lane == 64 + 2 * probes, 0.5, 0.0)
    aux = aux + jnp.dot(diag.astype(BF), put.astype(BF), preferred_element_type=F32)
    f = feats.astype(F32)
    rest = jnp.sum(f * f, axis=1, keepdims=True)
    for k in range(3):
        part = rest.astype(BF).astype(F32)
        aux = jnp.where(lane == 100 + k, part, aux)
        rest = rest - part
    return aux


def kernel(
    probes,
    amp_ref,
    lsq_ref,
    hidden_ref,
    proj_ref,
    alpha_ref,
    probe_ref,
    gh_ref,
    pp_ref,
    rows,
    cols,
    left,
    bias,
    moved,
    rsum,
    sbuf,
    rplus,
    rminus,
    row_send,
    row_recv,
    col_send,
    col_recv,
    part_send,
    part_recv,
    rs_send,
    rs_recv,
):
    pts, hid = hidden_ref.shape
    feat = proj_ref.shape[1]
    width = feat + AUX
    half, quarter = pts // 2, pts // 4
    n_rows, n_cols = rows.shape[0], cols.shape[0]

    r, c = lax.axis_index("row"), lax.axis_index("col")
    k, z, y_hi = r % 2, (r // 2) % NZ, r // (2 * NZ)
    x, y_lo = c // 2, c % 2
    y = y_hi * 2 + y_lo

    def dev(dx, dy, dz, flip=0):
        xx, yy, zz = (x + dx) % NX, (y + dy) % NY, (z + dz) % NZ
        kk = (1 - k) if flip else k
        return (((yy // 2) * NZ + zz) * 2 + kk, xx * 2 + yy % 2)

    xm, xp, ym, yp = dev(-1, 0, 0), dev(1, 0, 0), dev(0, -1, 0), dev(0, 1, 0)
    zm, zp, partner = dev(0, 0, -1), dev(0, 0, 1), dev(0, 0, 0, 1)

    barrier = pltpu.get_barrier_semaphore()
    for peer in (xm, xp, ym, yp, zm, zp, partner):
        pl.semaphore_signal(barrier, inc=1, device_id=peer, device_id_type=MESH)

    feats = jnp.dot(hidden_ref[...], proj_ref[...], preferred_element_type=F32).astype(BF)
    aux = aux_block(feats, alpha_ref[...], probe_ref[...], probes).astype(BF)
    for own in (rows, cols):
        own[0:pts, 0:feat] = feats
        own[0:pts, feat:width] = aux

    pl.semaphore_wait(barrier, 7)

    sends = []

    def send(src, dst, send_sem, recv_sem, to):
        copy = pltpu.make_async_remote_copy(
            src_ref=src,
            dst_ref=dst,
            send_sem=send_sem,
            recv_sem=recv_sem,
            device_id=to,
            device_id_type=MESH,
        )
        copy.start()
        sends.append(copy)

    def arrived(dst, recv_sem):
        pltpu.make_async_remote_copy(
            src_ref=dst,
            dst_ref=dst,
            send_sem=recv_sem,
            recv_sem=recv_sem,
            device_id=partner,
            device_id_type=MESH,
        ).wait_recv()

    n_row_sends = [0]

    def row_part(d, h):
        return rows.at[pl.ds(POS[d] * pts + h * half, half), :]

    def row_send_on(d, h, to_d, to):
        i = n_row_sends[0]
        n_row_sends[0] += 1
        send(row_part(d, h), row_part(to_d, h), row_send.at[i], row_recv.at[to_d, h], to)

    def col_part(core, dx, dy, q, n):
        start = ((core * NX + dx) * NY + dy) * pts + q * quarter
        return cols.at[pl.ds(start, n * quarter), :]

    n_col_sends = [0]

    def col_send_on(dx, dy, q, n, to_dx, to_dy, to):
        i = n_col_sends[0]
        n_col_sends[0] += 1
        send(
            col_part(0, dx, dy, q, n),
            col_part(0, to_dx, to_dy, q, n),
            col_send.at[i],
            col_recv.at[to_dx, to_dy, q],
            to,
        )

    def to_partner(dx, dy, h):
        send(
            col_part(0, dx, dy, 2 * h, 2),
            col_part(1, dx, dy, 2 * h, 2),
            part_send.at[dx, dy, h],
            part_recv.at[dx, dy, h],
            partner,
        )

    def at(h, a, b):
        return (a, b) if h == 0 else (b, a)

    def first_phase(h):
        minus, plus = ((xm, xp), (ym, yp))[h]
        col_send_on(0, 0, 2 * h, 2, *at(h, 1, 0), minus)
        col_send_on(0, 0, 2 * h, 2, *at(h, 3, 0), plus)

    def first_relay(h):
        minus, plus = ((xm, xp), (ym, yp))[h]
        col_send_on(*at(h, 1, 0), 2 * h, 1, *at(h, 2, 0), minus)
        col_send_on(*at(h, 3, 0), 2 * h + 1, 1, *at(h, 2, 0), plus)

    def second_phase(h, a):
        minus, plus = ((ym, yp), (xm, xp))[h]
        col_send_on(*at(h, a, 0), 2 * h, 2, *at(h, a, 1), minus)
        col_send_on(*at(h, a, 0), 2 * h, 2, *at(h, a, 3), plus)

    def second_relay(h, a):
        minus, plus = ((ym, yp), (xm, xp))[h]
        col_send_on(*at(h, a, 1), 2 * h, 1, *at(h, a, 2), minus)
        col_send_on(*at(h, a, 3), 2 * h + 1, 1, *at(h, a, 2), plus)

    def col_wait(h, a, b):
        dx, dy = at(h, a, b)
        arrived(col_part(0, dx, dy, 2 * h, 2), col_recv.at[dx, dy, 2 * h])

    def col_wait_quarters(h, a, b):
        dx, dy = at(h, a, b)
        for q in (2 * h, 2 * h + 1):
            arrived(col_part(0, dx, dy, q, 1), col_recv.at[dx, dy, q])

    for h in (0, 1):
        first_phase(h)
        row_send_on(0, h, 1, zm)
        row_send_on(0, h, 7, zp)
    for h in (0, 1):
        second_phase(h, 0)
        to_partner(0, 0, h)
    for h in (0, 1):
        for a in (1, 3):
            col_wait(h, a, 0)
        first_relay(h)
        for a in (1, 3):
            second_phase(h, a)
        for a in (1, 3):
            to_partner(*at(h, a, 0), h)
    for h in (0, 1):
        arrived(row_part(1, h), row_recv.at[1, h])
        row_send_on(1, h, 2, zm)
        arrived(row_part(7, h), row_recv.at[7, h])
        row_send_on(7, h, 6, zp)
    for h in (0, 1):
        for b in (1, 3):
            col_wait(h, 0, b)
        second_relay(h, 0)
        for b in (1, 3):
            to_partner(*at(h, 0, b), h)
    for h in (0, 1):
        col_wait_quarters(h, 2, 0)
        second_phase(h, 2)
        to_partner(*at(h, 2, 0), h)
    for h in (0, 1):
        arrived(row_part(2, h), row_recv.at[2, h])
        row_send_on(2, h, 3, zm)
        arrived(row_part(6, h), row_recv.at[6, h])
        row_send_on(6, h, 5, zp)
    for a in (1, 3, 2):
        for h in (0, 1):
            for b in (1, 3):
                col_wait(h, a, b)
            second_relay(h, a)
            for b in (1, 3):
                to_partner(*at(h, a, b), h)
        if a == 1:
            arrived(row_part(3, 0), row_recv.at[3, 0])
            row_send_on(3, 0, 4, zm)
            arrived(row_part(5, 1), row_recv.at[5, 1])
            row_send_on(5, 1, 4, zp)
    for a in (0, 1, 3, 2):
        for h in (0, 1):
            col_wait_quarters(h, a, 2)
            to_partner(*at(h, a, 2), h)
    for d, h in ((3, 1), (5, 0), (4, 0), (4, 1)):
        arrived(row_part(d, h), row_recv.at[d, h])

    scale = math.log2(math.e) / lsq_ref[0]

    lane = iota((n_rows, AUX), 1)
    raw = rows[:, feat:width].astype(F32)
    norms = jnp.where((lane >= 100) & (lane < 103), raw, 0.0)
    bias[...] = jnp.sum(norms, axis=1, keepdims=True) * (-0.5 * scale)
    turned = pltpu.roll(raw, 64, 1)
    left[...] = jnp.where((lane >= 64) & (lane <= 64 + 2 * probes), turned, 0.0).astype(BF)
    lane16 = iota((16, AUX), 1)
    picks = jnp.where((lane16 >= 100) & (lane16 < 103), 1.0, 0.0).astype(BF)

    for core in (1,):
        for dx in range(NX):
            for dy in range(NY):
                for h in (0, 1):
                    arrived(col_part(core, dx, dy, 2 * h, 2), part_recv.at[dx, dy, h])

    def group(g):
        m = 2 * pts
        rs = pl.ds(g * m, m)

        @pl.loop(0, n_cols // CHUNK)
        def _(j):
            cs = pl.ds(pl.multiple_of(j * CHUNK, CHUNK), CHUNK)
            col_f = cols[cs, 0:feat]
            col_a = cols[cs, feat:width]
            sq = lax.dot_general(picks, col_a, NT, preferred_element_type=F32)[0:1, :]
            inner = lax.dot_general(rows[rs, 0:feat], col_f, NT, preferred_element_type=F32)
            gmat = lax.dot_general(left[rs, :], col_a, NT, preferred_element_type=F32)
            expo = inner * scale + (bias[rs, :] + sq * (-0.5 * scale))
            weight = gmat * jnp.exp2(expo)
            total = weight[:, :128]
            for t in range(1, CHUNK // 128):
                total = total + weight[:, t * 128 : (t + 1) * 128]
            term = jnp.dot(weight.astype(BF), col_f, preferred_element_type=F32)

            @pl.when(j == 0)
            def _():
                rsum[...] = total
                moved[rs, :] = term

            @pl.when(j > 0)
            def _():
                rsum[...] += total
                moved[rs, :] += term

        rowsum = jnp.sum(rsum[...], axis=1, keepdims=True)
        moved[rs, :] = moved[rs, :] - rowsum * rows[rs, 0:feat].astype(F32)

    n_rs = [0]

    def pass_on(d, h, step, to, dst, arrival=None):
        rs = pl.ds(POS[d] * pts + h * half, half)
        hs = pl.ds(h * half, half)
        value = moved[rs, :]
        way = 0 if dst is rplus else 1
        if arrival is not None:
            ref = dst.at[arrival, hs, :]
            arrived(ref, rs_recv.at[way, arrival, h])
            value = value + dst[arrival, hs, :].astype(F32)
        sbuf[rs, :] = value.astype(BF)
        i = n_rs[0]
        n_rs[0] += 1
        send(sbuf.at[rs, :], dst.at[step, hs, :], rs_send.at[i], rs_recv.at[way, step, h], to)

    group(0)
    pass_on(4, 0, 0, zp, rplus)
    pass_on(4, 1, 0, zm, rminus)
    group(1)
    pass_on(3, 1, 1, zp, rplus)
    pass_on(5, 0, 1, zm, rminus)
    pass_on(3, 0, 1, zp, rplus, 0)
    pass_on(5, 1, 1, zm, rminus, 0)
    group(2)
    for h in (0, 1):
        pass_on(2, h, 2, zp, rplus, 1)
        pass_on(6, h, 2, zm, rminus, 1)
    group(3)
    for h in (0, 1):
        pass_on(1, h, 3, zp, rplus, 2)
        pass_on(7, h, 3, zm, rminus, 2)
    for h in (0, 1):
        hs = pl.ds(h * half, half)
        arrived(rplus.at[3, hs, :], rs_recv.at[0, 3, h])
        arrived(rminus.at[3, hs, :], rs_recv.at[1, 3, h])
    total = moved[0:pts, :] + rplus[3].astype(F32) + rminus[3].astype(F32)
    grad = (total * (2.0 * amp_ref[0] / lsq_ref[0])).astype(BF)
    gh_ref[...] = lax.dot_general(grad, proj_ref[...], NT, preferred_element_type=F32).astype(BF)
    pp_ref[...] = lax.dot_general(
        hidden_ref[...], grad, TN, preferred_element_type=F32
    ).astype(BF)
    for copy in sends:
        copy.wait_send()


def fused(hidden, projection, alpha, probe_pairs, amplitude, length_sq):
    pts, hid = hidden.shape
    feat = projection.shape[1]
    probes = probe_pairs.shape[1] // 2
    width = feat + AUX
    n_rows, n_cols = NZ * pts, 2 * NX * NY * pts
    half = pts // 2
    vmem = pl.BlockSpec(memory_space=pltpu.VMEM)
    smem = pl.BlockSpec(memory_space=pltpu.SMEM)
    dma = pltpu.SemaphoreType.DMA
    return pl.pallas_call(
        functools.partial(kernel, probes),
        out_shape=(
            jax.ShapeDtypeStruct((pts, hid), BF),
            jax.ShapeDtypeStruct((hid, feat), BF),
        ),
        in_specs=[smem, smem, vmem, vmem, vmem, vmem],
        out_specs=(vmem, vmem),
        scratch_shapes=[
            pltpu.VMEM((n_rows, width), BF),
            pltpu.VMEM((n_cols, width), BF),
            pltpu.VMEM((n_rows, AUX), BF),
            pltpu.VMEM((n_rows, 1), F32),
            pltpu.VMEM((n_rows, feat), F32),
            pltpu.VMEM((2 * pts, 128), F32),
            pltpu.VMEM((n_rows, feat), BF),
            pltpu.VMEM((4, pts, feat), BF),
            pltpu.VMEM((4, pts, feat), BF),
            dma((14,)),
            dma((NZ, 2)),
            dma((40,)),
            dma((NX, NY, 4)),
            dma((NX, NY, 2)),
            dma((NX, NY, 2)),
            dma((14,)),
            dma((2, 4, 2)),
        ],
        compiler_params=pltpu.CompilerParams(
            collective_id=0, has_side_effects=True, vmem_limit_bytes=56 << 20
        ),
        name="fused",
    )(amplitude, length_sq, hidden, projection, alpha[None, :], probe_pairs)


def per_device(hidden, projection, alpha, probe_pairs, amplitude, length_sq):
    grad_hidden, partial = fused(hidden, projection, alpha, probe_pairs, amplitude, length_sq)
    size = lax.axis_size("row")
    blocks = partial.reshape(size, partial.shape[0] // size, partial.shape[1])
    blocks = lax.all_to_all(blocks, "row", split_axis=0, concat_axis=0, tiled=True)
    share = blocks.astype(F32).sum(axis=0).astype(BF)
    size = lax.axis_size("col")
    every = lax.all_to_all(jnp.broadcast_to(share[None], (size, *share.shape)), "col", 0, 0, tiled=True)
    return grad_hidden, jnp.sum(every.astype(F32), axis=0)


def solution(mesh):
    placed = (P(("row", "col"), None), P(), P(("row", "col")), P(("row", "col"), None), P(), P())
    return jax.shard_map(
        per_device,
        mesh=mesh,
        in_specs=placed,
        out_specs=(P(("row", "col"), None), P("row", None)),
        check_vma=False,
    )
```

time: 356 us -> 103 us (0.29)
  the two profiles are of different devices: /device:TPU:1 before, /device:TPU:32 now
where the time goes in v1:
time: 103 us; the launch traced here: 102 us
  Pallas kernels  54.4 us (53%)
  blocking collectives  32 us (31%)
  waiting for transfers between devices  6.66 us (6%)
  starting transfers between devices  3.85 us (4%)
  local copies, waits for them, and re-layouts  2.79 us (3%)
  between operations  1.94 us (2%)
    pallas_call x1, Pallas kernels, fused(): pl.pallas_call(functools.partial(kernel, probes), out_shape=(jax.ShapeDty...  54.4 us
    all_to_all x1, blocking collectives, per_device(): lax.all_to_all(blocks, 'row', split_axis=0, concat_axis=0, tiled=True)  32 us
    all_to_all x1, waiting for transfers between devices, per_device(): lax.all_to_all(jnp.broadcast_to(share[None], (size, *share.shape)), 'col'...  6.66 us
    all_to_all x1, starting transfers between devices, per_device(): lax.all_to_all(jnp.broadcast_to(share[None], (size, *share.shape)), 'col'...  3.85 us
    unnamed x4, local copies, waits for them, and re-layouts  2.09 us
  transfers between devices with their start and end apart: 1, of which 1 were waited for; matrix products, arithmetic and copies ran while one was open for 0% of the time, Pallas kernels for 0%

profile of v1, /device:TPU:32, one launch (start us, length us, event | category | flops | bytes accessed | tf_op | source)
XLA Modules:
  0.0 102.4 jit_solution(818782174610585605)
XLA Ops:
  1.9 1.4 %copy.9.probe_ref = bf16[128,32]{1,0:T(8,128)(2,1)} copy(bf16[128,32]{0,1:T(8,128)(2,1)} %param.9) | data formatting | bytes 16384 | tf_op args[3]
  3.3 54.4 %fused.1 = (bf16[128,768]{1,0:T(8,128)(2,1)}, bf16[768,512]{1,0:T(8,128)(2,1)}) custom-call(f32[1]{0:T(128)S(6)} %copy.11.amp_ref, f32[1]{0:T(128)S(6)} %copy.12.lsq_ref, bf16[128,768]{1,0:T(8,128)(2,1)} %hidden_ref.1, bf16[768,512]{1,0:T(8,128)(2,1)} %proj_ref.1, bf16[1,128]{1,0:T(2,128)(2,1)} %bitcast.3, bf16[128,32]{1,0:T(8,128)(2,1)} %copy.9.probe_ref), custom_call_target="tpu_custom_call" | custom-call | tf_op jit(solution)/shard_map/fused/pallas_call | solution.py:357
  57.7 32.0 %all_to_all.10 = bf16[32,24,512]{2,1,0:T(8,128)(2,1)S(1)} all-to-all(bf16[32,24,512]{2,1,0:T(8,128)(2,1)} %bitcast.2), channel_id=1, replica_groups=mesh['row'=32,'col'=8] {'row'}, dimensions={0} | all-to-all | bytes 1572864 | tf_op jit(solution)/shard_map/all_to_all | solution.py:395
  89.7 0.1 reduce_sum.21
  89.8 0.7 broadcast_in_dim.10
  90.5 3.8 %all-to-all-start.1 = ((bf16[8,24,512]{2,1,0:T(8,128)(2,1)}), bf16[8,24,512]{2,1,0:T(8,128)(2,1)S(1)}, u32[]{:S(2)}, u32[]{:S(2)}) async-start(bf16[8,24,512]{2,1,0:T(8,128)(2,1)} %broadcast_in_dim.10), calls=%async_computation.1 | async-start | bytes 393216 | tf_op jit(solution)/shard_map/all_to_all | solution.py:398
  94.4 0.0 copy-start
  94.4 6.7 %all-to-all-done.1 = bf16[8,24,512]{2,1,0:T(8,128)(2,1)S(1)} async-done(((bf16[8,24,512]{2,1,0:T(8,128)(2,1)}), bf16[8,24,512]{2,1,0:T(8,128)(2,1)S(1)}, u32[]{:S(2)}, u32[]{:S(2)}) %all-to-all-start.1) | async-done | bytes 196640 | tf_op jit(solution)/shard_map/all_to_all | solution.py:398
  101.0 0.6 convert_reduce_fusion
  101.7 0.0 copy-done
  101.7 0.7 copy.13
Async XLA Ops:
  90.5 10.5 %all-to-all-start.1 = ((bf16[8,24,512]{2,1,0:T(8,128)(2,1)}), bf16[8,24,512]{2,1,0:T(8,128)(2,1)S(1)}, u32[]{:S(2)}, u32[]{:S(2)}) async-start(bf16[8,24,512]{2,1,0:T(8,128)(2,1)} %broadcast_in_dim.10), calls=%async_computation.1 | async-start | bytes 393216 | tf_op jit(solution)/shard_map/all_to_all | solution.py:398
  94.4 7.3 %copy-start = (bf16[128,768]{1,0:T(8,128)(2,1)S(1)}, bf16[128,768]{1,0:T(8,128)(2,1)}, u32[]{:S(2)}) copy-start(bf16[128,768]{1,0:T(8,128)(2,1)} %get-tuple-element.8) | copy-start | bytes 589828

commit v2 on v1

--- a/solution.py
+++ b/solution.py
@@ -23,13 +23,13 @@
     return lax.broadcasted_iota(jnp.int32, shape, dim)
 
 
-def aux_block(feats, alpha_row, probe, probes):
+def aux_block(feats, alpha_row, probe_t, probes):
     points = feats.shape[0]
     src, lane = iota((2 * probes, AUX), 0), iota((2 * probes, AUX), 1)
     scale = 1.0 / (4 * probes)
     swapped = jnp.where(src < probes, src + probes, src - probes)
     pick = jnp.where(lane == src, 1.0, 0.0) + jnp.where(lane - 64 == swapped, -scale, 0.0)
-    aux = jnp.dot(probe, pick.astype(BF), preferred_element_type=F32)
+    aux = lax.dot_general(probe_t, pick.astype(BF), TN, preferred_element_type=F32)
     spread = jnp.broadcast_to(alpha_row.astype(F32), (points, points))
     diag = jnp.where(iota((points, points), 0) == iota((points, points), 1), spread, 0.0)
     lane = iota((points, AUX), 1)
@@ -53,7 +53,7 @@
     alpha_ref,
     probe_ref,
     gh_ref,
-    pp_ref,
+    gp_ref,
     rows,
     cols,
     left,
@@ -71,6 +71,22 @@
     part_recv,
     rs_send,
     rs_recv,
+    other_hid,
+    gbuf,
+    pbuf,
+    prec,
+    zbuf,
+    zrec,
+    fbuf,
+    frec,
+    pair_send,
+    pair_recv,
+    p_send,
+    p_recv,
+    z_send,
+    z_recv,
+    f_send,
+    f_recv,
 ):
     pts, hid = hidden_ref.shape
     feat = proj_ref.shape[1]
@@ -195,6 +211,7 @@
         for q in (2 * h, 2 * h + 1):
             arrived(col_part(0, dx, dy, q, 1), col_recv.at[dx, dy, q])
 
+    send(hidden_ref, other_hid, pair_send.at[0], pair_recv.at[0], partner)
     for h in (0, 1):
         first_phase(h)
         row_send_on(0, h, 1, zm)
@@ -206,6 +223,7 @@
         for a in (1, 3):
             col_wait(h, a, 0)
         first_relay(h)
+    for h in (0, 1):
         for a in (1, 3):
             second_phase(h, a)
         for a in (1, 3):
@@ -336,12 +354,114 @@
         arrived(rminus.at[3, hs, :], rs_recv.at[1, 3, h])
     total = moved[0:pts, :] + rplus[3].astype(F32) + rminus[3].astype(F32)
     grad = (total * (2.0 * amp_ref[0] / lsq_ref[0])).astype(BF)
+    gbuf[0] = grad
+
+    proj_own = lax.dot_general(hidden_ref[...], grad, TN, preferred_element_type=F32)
+    send(gbuf.at[0], gbuf.at[1], pair_send.at[1], pair_recv.at[1], partner)
+    arrived(other_hid, pair_recv.at[0])
+    arrived(gbuf.at[1], pair_recv.at[1])
+    terms = proj_own + lax.dot_general(other_hid[...], gbuf[1], TN, preferred_element_type=F32)
+    size = hid // (4 * NZ)
+    for hi in range(2):
+        for zz in range(NZ):
+            for core in range(2):
+                start = ((hi * NZ + zz) * 2 + core) * size
+                pbuf[hi, core, zz] = terms[start : start + size, :].astype(BF)
+
+    zs = pl.ds(k * (NZ // 2), NZ // 2)
+
+    def portion(xx, yy):
+        return yy // 2, yy % 2, zs, slice(None), pl.ds(pl.multiple_of(xx * 128, 128), 128)
+
+    for dx in range(NX):
+        for dy in range(NY):
+            if dx or dy:
+                to = ((NX - dx) % NX, (NY - dy) % NY)
+                send(
+                    pbuf.at[portion((x + dx) % NX, (y + dy) % NY)],
+                    prec.at[to[0], to[1]],
+                    p_send.at[dx, dy],
+                    p_recv.at[to[0], to[1]],
+                    dev(dx, dy, 0),
+                )
     gh_ref[...] = lax.dot_general(grad, proj_ref[...], NT, preferred_element_type=F32).astype(BF)
-    pp_ref[...] = lax.dot_general(
-        hidden_ref[...], grad, TN, preferred_element_type=F32
-    ).astype(BF)
+    share = pbuf[portion(x, y)].astype(F32)
+    for dx in range(NX):
+        for dy in range(NY):
+            if dx or dy:
+                arrived(prec.at[dx, dy], p_recv.at[dx, dy])
+                share = share + prec[dx, dy].astype(F32)
+    zbuf[...] = share.astype(BF)
+
+    gathers = k == z // (NZ // 2)
+    later = []
+
+    def send_if(cond, src, dst, send_sem, recv_sem, to):
+        copy = pltpu.make_async_remote_copy(
+            src_ref=src,
+            dst_ref=dst,
+            send_sem=send_sem,
+            recv_sem=recv_sem,
+            device_id=to,
+            device_id_type=MESH,
+        )
+
+        @pl.when(cond)
+        def _():
+            copy.start()
+
+        later.append((cond, copy))
+
+    for dz in range(1, NZ):
+        zz = (z + dz) % NZ
+        send_if(
+            zz // (NZ // 2) == k,
+            zbuf.at[zz % (NZ // 2)],
+            zrec.at[NZ - dz],
+            z_send.at[dz],
+            z_recv.at[NZ - dz],
+            dev(0, 0, dz),
+        )
+
+    @pl.when(gathers)
+    def _():
+        total = zbuf[z % (NZ // 2)].astype(F32)
+        for dz in range(1, NZ):
+            arrived(zrec.at[dz], z_recv.at[dz])
+            total = total + zrec[dz].astype(F32)
+        fbuf[...] = total
+
+    mine = y_lo == k
+    for dx in range(NX):
+        for flip in range(2):
+            xx, yy = (x + dx) % NX, y_hi * 2 + (y_lo if flip == 0 else 1 - y_lo)
+            to = ((y_hi * NZ + z) * 2 + y_lo, xx * 2 + yy % 2)
+            cond = gathers if dx or flip else gathers & jnp.logical_not(mine)
+            slot = (NX - dx) % NX
+            send_if(cond, fbuf, frec.at[slot], f_send.at[dx, flip], f_recv.at[slot], to)
+
+    @pl.when(gathers & mine)
+    def _():
+        frec[0] = fbuf[...]
+
+    for dx in range(NX):
+        if dx == 0:
+
+            @pl.when(jnp.logical_not(gathers & mine))
+            def _():
+                arrived(frec.at[0], f_recv.at[0])
+
+        else:
+            arrived(frec.at[dx], f_recv.at[dx])
+        gp_ref[:, pl.ds(pl.multiple_of((x + dx) % NX * 128, 128), 128)] = frec[dx]
+
     for copy in sends:
         copy.wait_send()
+    for cond, copy in later:
+
+        @pl.when(cond)
+        def _():
+            copy.wait_send()
 
 
 def fused(hidden, projection, alpha, probe_pairs, amplitude, length_sq):
@@ -358,7 +478,7 @@
         functools.partial(kernel, probes),
         out_shape=(
             jax.ShapeDtypeStruct((pts, hid), BF),
-            jax.ShapeDtypeStruct((hid, feat), BF),
+            jax.ShapeDtypeStruct((hid // (4 * NZ), feat), F32),
         ),
         in_specs=[smem, smem, vmem, vmem, vmem, vmem],
         out_specs=(vmem, vmem),
@@ -380,23 +500,32 @@
             dma((NX, NY, 2)),
             dma((14,)),
             dma((2, 4, 2)),
+            pltpu.VMEM((pts, hid), BF),
+            pltpu.VMEM((2, pts, feat), BF),
+            pltpu.VMEM((2, 2, NZ, hid // (4 * NZ), feat), BF),
+            pltpu.VMEM((NX, NY, NZ // 2, hid // (4 * NZ), 128), BF),
+            pltpu.VMEM((NZ // 2, hid // (4 * NZ), 128), BF),
+            pltpu.VMEM((NZ, hid // (4 * NZ), 128), BF),
+            pltpu.VMEM((hid // (4 * NZ), 128), F32),
+            pltpu.VMEM((NX, hid // (4 * NZ), 128), F32),
+            dma((2,)),
+            dma((2,)),
+            dma((NX, NY)),
+            dma((NX, NY)),
+            dma((NZ,)),
+            dma((NZ,)),
+            dma((NX, 2)),
+            dma((NX,)),
         ],
         compiler_params=pltpu.CompilerParams(
             collective_id=0, has_side_effects=True, vmem_limit_bytes=56 << 20
         ),
         name="fused",
-    )(amplitude, length_sq, hidden, projection, alpha[None, :], probe_pairs)
+    )(amplitude, length_sq, hidden, projection, alpha[None, :], probe_pairs.T)
 
 
 def per_device(hidden, projection, alpha, probe_pairs, amplitude, length_sq):
-    grad_hidden, partial = fused(hidden, projection, alpha, probe_pairs, amplitude, length_sq)
-    size = lax.axis_size("row")
-    blocks = partial.reshape(size, partial.shape[0] // size, partial.shape[1])
-    blocks = lax.all_to_all(blocks, "row", split_axis=0, concat_axis=0, tiled=True)
-    share = blocks.astype(F32).sum(axis=0).astype(BF)
-    size = lax.axis_size("col")
-    every = lax.all_to_all(jnp.broadcast_to(share[None], (size, *share.shape)), "col", 0, 0, tiled=True)
-    return grad_hidden, jnp.sum(every.astype(F32), axis=0)
+    return fused(hidden, projection, alpha, probe_pairs, amplitude, length_sq)
 
 
 def solution(mesh):

time: 103 us -> 78.1 us (0.76)
  the two profiles are of different devices: /device:TPU:32 before, /device:TPU:1 now
where the time goes in v2:
time: 78.1 us; the launch traced here: 77.9 us
  Pallas kernels  73.7 us (94%)
  local copies, waits for them, and re-layouts  2.25 us (3%)
  between operations  1.94 us (2%)
    pallas_call x1, Pallas kernels, fused(): pl.pallas_call(functools.partial(kernel, probes), out_shape=(jax.ShapeDty...  73.7 us
    unnamed x4, local copies, waits for them, and re-layouts  2.25 us

profile of v2, /device:TPU:1, one launch (start us, length us, event | category | flops | bytes accessed | tf_op | source)
XLA Modules:
  0.0 77.9 jit_solution(14202317606442923630)
XLA Ops:
  1.9 73.7 %fused.1 = (bf16[128,768]{1,0:T(8,128)(2,1)}, f32[24,512]{1,0:T(8,128)}) custom-call(f32[1]{0:T(128)S(6)} %copy.10.amp_ref, f32[1]{0:T(128)S(6)} %copy.11.lsq_ref, bf16[128,768]{1,0:T(8,128)(2,1)} %hidden_ref.1, bf16[768,512]{1,0:T(8,128)(2,1)} %proj_ref.1, bf16[1,128]{1,0:T(2,128)(2,1)} %bitcast.3, bf16[32,128]{1,0:T(8,128)(2,1)} %bitcast.2), custom_call_target="tpu_custom_call" | custom-call | tf_op jit(solution)/shard_map/fused/pallas_call | solution.py:477
  75.7 0.0 copy-start
  75.7 1.6 %copy.12 = bf16[128,768]{1,0:T(8,128)(2,1)} copy(bf16[128,768]{1,0:T(8,128)(2,1)} %get-tuple-element.4) | data formatting | bytes 393216
  77.3 0.0 copy-done
  77.3 0.6 copy.13
Async XLA Ops:
  75.7 1.6 %copy-start = (f32[24,512]{1,0:T(8,128)S(1)}, f32[24,512]{1,0:T(8,128)}, u32[]{:S(2)}) copy-start(f32[24,512]{1,0:T(8,128)} %get-tuple-element.5) | copy-start | bytes 147460

commit v3 on v2

v3 whole, which is shorter than its diff:
```python
import functools
import math

import jax
import jax.numpy as jnp
from jax import lax
from jax.experimental import pallas as pl
from jax.experimental.pallas import tpu as pltpu
from jax.sharding import PartitionSpec as P

MESH = pl.DeviceIdType.MESH
NT = (((1,), (1,)), ((), ()))
TN = (((0,), (0,)), ((), ()))
BF, F32 = jnp.bfloat16, jnp.float32

NX, NY, NZ = 4, 4, 8
AUX = 128
POS = {0: 0, 4: 1, 3: 2, 5: 3, 2: 4, 6: 5, 1: 6, 7: 7}
GROUPS = 4
CHUNK = 1024
PARTS = 4
SLOTS = [
    (0, 0, 0), (1, 0, 0), (0, 0, 1), (0, 0, 3), (0, 1, 0), (0, 3, 0), (1, 0, 1), (1, 0, 3),
    (1, 1, 0), (1, 3, 0), (0, 1, 1), (0, 1, 3), (0, 3, 1), (0, 3, 3), (1, 1, 1), (0, 0, 2),
    (0, 2, 0), (1, 1, 3), (1, 3, 1), (1, 3, 3), (1, 0, 2), (1, 2, 0), (0, 1, 2), (0, 2, 1),
    (0, 2, 3), (0, 3, 2), (1, 1, 2), (1, 2, 1), (1, 2, 3), (1, 3, 2), (0, 2, 2), (1, 2, 2),
]
PLAN = [
    ("r", 0, 0, 1, 0), ("r", 0, 0, 7, 1), ("r", 0, 1, 1, 0), ("r", 0, 1, 7, 1), ("r", 0, 2, 1, 0), ("r", 0, 2, 7, 1),
    ("r", 0, 3, 1, 0), ("r", 0, 3, 7, 1), ("c", 0, 0, 0, 1, 0, 0), ("c", 0, 0, 1, 1, 0, 0), ("c", 0, 0, 2, 0, 1, 2),
    ("c", 0, 0, 3, 0, 1, 2), ("c", 0, 0, 0, 3, 0, 1), ("c", 0, 0, 1, 3, 0, 1), ("c", 0, 0, 2, 0, 3, 3),
    ("c", 0, 0, 3, 0, 3, 3), ("c", 0, 0, 0, 0, 1, 2), ("c", 0, 0, 1, 0, 1, 2), ("c", 0, 0, 2, 1, 0, 0),
    ("c", 0, 0, 3, 1, 0, 0), ("c", 0, 0, 0, 0, 3, 3), ("c", 0, 0, 1, 0, 3, 3), ("c", 0, 0, 2, 3, 0, 1),
    ("c", 0, 0, 3, 3, 0, 1), ("p", 0, 0, 0), ("p", 0, 0, 1), ("wp", 0, 0, 0), ("wp", 0, 0, 1), ("wc", 0, 1, 2),
    ("c", 0, 1, 2, 0, 2, 2), ("c", 0, 1, 2, 1, 1, 0), ("c", 0, 1, 2, 3, 1, 1), ("wc", 0, 3, 2),
    ("c", 0, 3, 2, 1, 3, 0), ("c", 0, 3, 2, 3, 3, 1), ("wc", 1, 0, 0), ("c", 1, 0, 0, 2, 0, 0),
    ("c", 1, 0, 0, 1, 1, 2), ("c", 1, 0, 0, 1, 3, 3), ("wc", 3, 0, 0), ("c", 3, 0, 0, 3, 1, 2),
    ("c", 3, 0, 0, 3, 3, 3), ("wr", 1, 0), ("r", 1, 0, 2, 0), ("wr", 7, 0), ("r", 7, 0, 6, 1), ("wc", 0, 1, 3),
    ("c", 0, 1, 3, 1, 1, 0), ("c", 0, 1, 3, 3, 1, 1), ("p", 0, 1, 1), ("wc", 0, 3, 3), ("c", 0, 3, 3, 0, 2, 3),
    ("c", 0, 3, 3, 1, 3, 0), ("c", 0, 3, 3, 3, 3, 1), ("p", 0, 3, 1), ("wc", 1, 0, 1), ("c", 1, 0, 1, 1, 1, 2),
    ("c", 1, 0, 1, 1, 3, 3), ("p", 1, 0, 0), ("wc", 3, 0, 1), ("c", 3, 0, 1, 2, 0, 1), ("c", 3, 0, 1, 3, 1, 2),
    ("c", 3, 0, 1, 3, 3, 3), ("p", 3, 0, 0), ("wr", 1, 1), ("r", 1, 1, 2, 0), ("wr", 7, 1), ("r", 7, 1, 6, 1),
    ("wc", 0, 1, 0), ("c", 0, 1, 0, 0, 2, 2), ("wc", 0, 3, 0), ("wc", 1, 0, 2), ("c", 1, 0, 2, 2, 0, 0),
    ("wc", 3, 0, 2), ("wp", 0, 1, 1), ("wp", 0, 3, 1), ("wc", 0, 1, 1), ("p", 0, 1, 0), ("wc", 0, 3, 1),
    ("c", 0, 3, 1, 0, 2, 3), ("p", 0, 3, 0), ("wc", 1, 0, 3), ("p", 1, 0, 1), ("wc", 3, 0, 3),
    ("c", 3, 0, 3, 2, 0, 1), ("p", 3, 0, 1), ("wp", 1, 0, 0), ("wr", 1, 2), ("r", 1, 2, 2, 0), ("wr", 7, 2),
    ("r", 7, 2, 6, 1), ("wp", 3, 0, 0), ("wc", 0, 2, 2), ("c", 0, 2, 2, 1, 2, 0), ("c", 0, 2, 2, 3, 2, 1),
    ("wc", 1, 1, 2), ("c", 1, 1, 2, 2, 1, 0), ("wc", 1, 3, 0), ("wc", 3, 1, 2), ("wp", 0, 1, 0), ("wr", 1, 3),
    ("r", 1, 3, 2, 0), ("wr", 7, 3), ("r", 7, 3, 6, 1), ("wp", 0, 3, 0), ("G", 3), ("g", 3, 0), ("wr", 2, 0),
    ("r", 2, 0, 3, 0), ("wr", 6, 0), ("r", 6, 0, 5, 1), ("wc", 0, 2, 3), ("c", 0, 2, 3, 1, 2, 0),
    ("c", 0, 2, 3, 3, 2, 1), ("p", 0, 2, 1), ("wc", 2, 0, 0), ("c", 2, 0, 0, 2, 1, 2), ("c", 2, 0, 0, 2, 3, 3),
    ("wc", 1, 1, 0), ("c", 1, 1, 0, 1, 2, 2), ("wc", 1, 3, 2), ("c", 1, 3, 2, 2, 3, 0), ("wc", 3, 3, 0),
    ("wc", 3, 3, 2), ("wc", 3, 1, 0), ("c", 3, 1, 0, 3, 2, 2), ("wc", 3, 1, 3), ("c", 3, 1, 3, 2, 1, 1),
    ("p", 3, 1, 1), ("wp", 1, 0, 1), ("wc", 1, 1, 1), ("p", 1, 1, 0), ("wc", 1, 1, 3), ("p", 1, 1, 1),
    ("wc", 1, 3, 1), ("c", 1, 3, 1, 1, 2, 3), ("p", 1, 3, 0), ("wc", 3, 3, 3), ("c", 3, 3, 3, 2, 3, 1),
    ("p", 3, 3, 1), ("wp", 3, 0, 1), ("wr", 2, 1), ("r", 2, 1, 3, 0), ("wr", 6, 1), ("r", 6, 1, 5, 1),
    ("wc", 2, 0, 1), ("c", 2, 0, 1, 2, 1, 2), ("c", 2, 0, 1, 2, 3, 3), ("p", 2, 0, 0), ("wc", 1, 3, 3),
    ("p", 1, 3, 1), ("wc", 3, 1, 1), ("p", 3, 1, 0), ("wc", 3, 3, 1), ("c", 3, 3, 1, 3, 2, 3), ("p", 3, 3, 0),
    ("wp", 0, 2, 1), ("wp", 3, 1, 1), ("wr", 2, 2), ("r", 2, 2, 3, 0), ("wr", 6, 2), ("r", 6, 2, 5, 1),
    ("wp", 1, 1, 0), ("wc", 0, 2, 0), ("wc", 0, 2, 1), ("p", 0, 2, 0), ("wc", 2, 0, 2), ("wc", 2, 0, 3),
    ("p", 2, 0, 1), ("wp", 1, 1, 1), ("g", 3, 1), ("wr", 2, 3), ("r", 2, 3, 3, 0), ("wr", 6, 3), ("r", 6, 3, 5, 1),
    ("wc", 1, 2, 2), ("c", 1, 2, 2, 2, 2, 0), ("wc", 3, 2, 2), ("wc", 2, 1, 0), ("c", 2, 1, 0, 2, 2, 2),
    ("wc", 2, 3, 0), ("wp", 1, 3, 0), ("wp", 3, 3, 1), ("wp", 2, 0, 0), ("wp", 1, 3, 1), ("wp", 3, 1, 0), ("G", 2),
    ("g", 2, 0), ("wr", 3, 0), ("r", 3, 0, 4, 0), ("wr", 5, 0), ("wc", 3, 2, 3), ("c", 3, 2, 3, 2, 2, 1),
    ("p", 3, 2, 1), ("wc", 1, 2, 3), ("p", 1, 2, 1), ("wc", 2, 3, 1), ("c", 2, 3, 1, 2, 2, 3), ("p", 2, 3, 0),
    ("wc", 2, 1, 2), ("wr", 3, 1), ("r", 3, 1, 4, 0), ("wr", 5, 1), ("wc", 1, 2, 0), ("wc", 1, 2, 1), ("p", 1, 2, 0),
    ("wc", 2, 1, 3), ("p", 2, 1, 1), ("wc", 3, 2, 0), ("wc", 2, 3, 2), ("wc", 2, 3, 3), ("p", 2, 3, 1),
    ("wp", 3, 3, 0), ("wp", 0, 2, 0), ("wp", 2, 0, 1), ("g", 2, 1), ("wr", 3, 2), ("wr", 5, 2), ("r", 5, 2, 4, 1),
    ("wc", 2, 1, 1), ("p", 2, 1, 0), ("wc", 3, 2, 1), ("p", 3, 2, 0), ("wc", 2, 2, 2), ("wc", 2, 2, 0),
    ("wp", 3, 2, 1), ("wp", 1, 2, 1), ("g", 2, 2), ("wr", 3, 3), ("wr", 5, 3), ("r", 5, 3, 4, 1), ("wp", 2, 3, 0),
    ("wp", 1, 2, 0), ("wp", 2, 1, 1), ("wp", 2, 3, 1), ("wp", 2, 1, 0), ("G", 1), ("g", 1, 0), ("wr", 4, 0),
    ("wc", 2, 2, 3), ("p", 2, 2, 1), ("wc", 2, 2, 1), ("p", 2, 2, 0), ("wp", 3, 2, 0), ("g", 1, 1), ("wr", 4, 1),
    ("wr", 4, 2), ("wp", 2, 2, 1), ("g", 1, 2), ("wr", 4, 3), ("wp", 2, 2, 0), ("G", 0), ("g", 0, 0), ("g", 0, 1),
    ("g", 0, 2), ("g", 0, 3), ("F", 0), ("R", 4, 0), ("R", 4, 1), ("R", 4, 2), ("R", 4, 3), ("g", 1, 3), ("F", 1),
    ("R", 3, 2), ("R", 3, 3), ("R", 5, 0), ("R", 5, 1), ("g", 2, 3), ("F", 2), ("R", 3, 0), ("R", 3, 1), ("R", 5, 2),
    ("R", 5, 3), ("g", 3, 2), ("R", 2, 2), ("R", 2, 3), ("R", 6, 0), ("R", 6, 1), ("g", 3, 3), ("F", 3), ("R", 2, 0),
    ("R", 2, 1), ("R", 6, 2), ("R", 6, 3), ("R", 1, 2), ("R", 7, 0), ("R", 1, 3), ("R", 7, 1), ("R", 1, 0),
    ("R", 7, 2), ("R", 1, 1), ("R", 7, 3),
]


def iota(shape, dim):
    return lax.broadcasted_iota(jnp.int32, shape, dim)


def aux_block(feats, alpha_row, probe_t, probes):
    points = feats.shape[0]
    src, lane = iota((2 * probes, AUX), 0), iota((2 * probes, AUX), 1)
    scale = 1.0 / (4 * probes)
    swapped = jnp.where(src < probes, src + probes, src - probes)
    pick = jnp.where(lane == src, 1.0, 0.0) + jnp.where(lane - 64 == swapped, -scale, 0.0)
    aux = lax.dot_general(probe_t, pick.astype(BF), TN, preferred_element_type=F32)
    spread = jnp.broadcast_to(alpha_row.astype(F32), (points, points))
    diag = jnp.where(iota((points, points), 0) == iota((points, points), 1), spread, 0.0)
    lane = iota((points, AUX), 1)
    put = jnp.where(lane == 2 * probes, 1.0, 0.0) + jnp.where(lane == 64 + 2 * probes, 0.5, 0.0)
    aux = aux + jnp.dot(diag.astype(BF), put.astype(BF), preferred_element_type=F32)
    f = feats.astype(F32)
    rest = jnp.sum(f * f, axis=1, keepdims=True)
    for k in range(3):
        part = rest.astype(BF).astype(F32)
        aux = jnp.where(lane == 100 + k, part, aux)
        rest = rest - part
    return aux


def kernel(
    probes,
    amp_ref,
    lsq_ref,
    hidden_ref,
    proj_ref,
    alpha_ref,
    probe_ref,
    gh_ref,
    gp_ref,
    rows,
    row_feat,
    cols,
    left,
    bias,
    moved,
    rsum,
    sbuf,
    rplus,
    rminus,
    terms,
    pbuf,
    xrec,
    prec,
    zbuf,
    zrec,
    fbuf,
    frec,
    row_send,
    row_recv,
    col_send,
    col_recv,
    part_send,
    part_recv,
    rs_send,
    rs_recv,
    pair_send,
    pair_recv,
    p_send,
    p_recv,
    z_send,
    z_recv,
    f_send,
    f_recv,
):
    pts, hid = hidden_ref.shape
    feat = proj_ref.shape[1]
    width = feat + AUX
    half, quarter, piece = pts // 2, pts // 4, pts // PARTS
    m = 2 * pts

    r, c = lax.axis_index("row"), lax.axis_index("col")
    k, z, y_hi = r % 2, (r // 2) % NZ, r // (2 * NZ)
    x, y_lo = c // 2, c % 2
    y = y_hi * 2 + y_lo

    def dev(dx, dy, dz, flip=0):
        xx, yy, zz = (x + dx) % NX, (y + dy) % NY, (z + dz) % NZ
        kk = (1 - k) if flip else k
        return (((yy // 2) * NZ + zz) * 2 + kk, xx * 2 + yy % 2)

    plane = (dev(-1, 0, 0), dev(1, 0, 0), dev(0, -1, 0), dev(0, 1, 0))
    line = (dev(0, 0, -1), dev(0, 0, 1))
    partner = dev(0, 0, 0, 1)

    barrier = pltpu.get_barrier_semaphore()
    for peer in (*plane, *line, partner):
        pl.semaphore_signal(barrier, inc=1, device_id=peer, device_id_type=MESH)

    feats = jnp.dot(hidden_ref[...], proj_ref[...], preferred_element_type=F32).astype(BF)
    aux = aux_block(feats, alpha_ref[...], probe_ref[...], probes).astype(BF)
    own = pl.ds(SLOTS.index((0, 0, 0)) * pts, pts)
    cols[own, 0:feat] = feats
    cols[own, feat:width] = aux
    own = pl.ds(POS[0] * pts, pts)
    rows[own, 0:hid] = hidden_ref[...]
    rows[own, hid : hid + AUX] = aux

    pl.semaphore_wait(barrier, 7)

    sends = []
    used = {}

    def send(src, dst, sems, recv_sem, to):
        if isinstance(sems, tuple):
            sem = sems[0].at[sems[1:]]
        else:
            sem = sems.at[used.setdefault(id(sems), 0)]
            used[id(sems)] += 1
        copy = pltpu.make_async_remote_copy(
            src_ref=src,
            dst_ref=dst,
            send_sem=sem,
            recv_sem=recv_sem,
            device_id=to,
            device_id_type=MESH,
        )
        copy.start()
        sends.append(copy)

    def arrived(dst, recv_sem):
        pltpu.make_async_remote_copy(
            src_ref=dst,
            dst_ref=dst,
            send_sem=recv_sem,
            recv_sem=recv_sem,
            device_id=partner,
            device_id_type=MESH,
        ).wait_recv()

    def row_part(d, q):
        return rows.at[pl.ds(POS[d] * pts + q * quarter, quarter), :]

    def col_part(core, dx, dy, q, n):
        start = SLOTS.index((core, dx, dy)) * pts + q * quarter
        return cols.at[pl.ds(start, n * quarter), :]

    scale = math.log2(math.e) / lsq_ref[0]
    final = 2.0 * amp_ref[0] / lsq_ref[0]
    lane16 = iota((16, AUX), 1)
    picks = jnp.where((lane16 >= 100) & (lane16 < 103), 1.0, 0.0).astype(BF)

    def prepare(g):
        rs = pl.ds(g * m, m)
        row_feat[rs, :] = jnp.dot(
            rows[rs, 0:hid], proj_ref[...], preferred_element_type=F32
        ).astype(BF)
        lane = iota((m, AUX), 1)
        raw = rows[rs, hid : hid + AUX].astype(F32)
        norms = jnp.where((lane >= 100) & (lane < 103), raw, 0.0)
        bias[rs, :] = jnp.sum(norms, axis=1, keepdims=True) * (-0.5 * scale)
        turned = pltpu.roll(raw, 64, 1)
        factors = jnp.where((lane >= 64) & (lane <= 64 + 2 * probes), turned, 0.0)
        left[rs, :] = factors.astype(BF)

    def chunk(g, first, n, fresh):
        rs, count = pl.ds(g * m, m), n * CHUNK
        cs = pl.ds(first * CHUNK, count)
        col_f = cols[cs, 0:feat]
        col_a = cols[cs, feat:width]
        sq = lax.dot_general(picks, col_a, NT, preferred_element_type=F32)[0:1, :]
        inner = lax.dot_general(row_feat[rs, :], col_f, NT, preferred_element_type=F32)
        gmat = lax.dot_general(left[rs, :], col_a, NT, preferred_element_type=F32)
        expo = inner * scale + (bias[rs, :] + sq * (-0.5 * scale))
        weight = gmat * jnp.exp2(expo)
        total = weight[:, :128]
        for t in range(1, count // 128):
            total = total + weight[:, t * 128 : (t + 1) * 128]
        term = jnp.dot(weight.astype(BF), col_f, preferred_element_type=F32)
        if fresh:
            rsum[rs, :] = total
            moved[rs, :] = term
        else:
            rsum[rs, :] += total
            moved[rs, :] += term

    def finish(g, fresh):
        rs = pl.ds(g * m, m)
        rowsum = jnp.sum(rsum[rs, :], axis=1, keepdims=True)
        value = moved[rs, :] - rowsum * row_feat[rs, :].astype(F32)
        moved[rs, :] = value
        term = lax.dot_general(rows[rs, 0:hid], value.astype(BF), TN, preferred_element_type=F32)
        terms[...] = term if fresh else terms[...] + term

    def pass_on(d, i):
        up = d < 4 or (d == 4 and i < PARTS // 2)
        dst, way = (rplus, 0) if up else (rminus, 1)
        step = 4 - d if up else d - 4
        rs = pl.ds(POS[d] * pts + i * piece, piece)
        ps = pl.ds(i * piece, piece)
        value = moved[rs, :]
        if step > 1 or (step == 1 and up == (i < PARTS // 2)):
            arrived(dst.at[step - 1, ps, :], rs_recv.at[way, step - 1, i])
            value = value + dst[step - 1, ps, :].astype(F32)
        sbuf[rs, :] = value.astype(BF)
        send(sbuf.at[rs, :], dst.at[step, ps, :], rs_send, rs_recv.at[way, step, i], line[up])

    def row_step(op):
        if op[0] == "wr":
            arrived(row_part(*op[1:]), row_recv.at[op[1:]])
        else:
            d, q, to_d, up = op[1:]
            send(row_part(d, q), row_part(to_d, q), row_send, row_recv.at[to_d, q], line[up])

    def col_step(op):
        if op[0] == "wc":
            arrived(col_part(0, *op[1:], 1), col_recv.at[op[1:]])
        elif op[0] == "c":
            dx, dy, q, to_dx, to_dy, way = op[1:]
            dst = col_part(0, to_dx, to_dy, q, 1)
            send(col_part(0, dx, dy, q, 1), dst, col_send, col_recv.at[to_dx, to_dy, q], plane[way])
        else:
            dx, dy, h = op[1:]
            dst = col_part(1, dx, dy, 2 * h, 2)
            if op[0] == "wp":
                arrived(dst, part_recv.at[dx, dy, h])
            else:
                src = col_part(0, dx, dy, 2 * h, 2)
                send(src, dst, part_send, part_recv.at[dx, dy, h], partner)

    seen, finished = set(), 0
    at = 0
    while finished < GROUPS:
        op = PLAN[at]
        at += 1
        if op[0] == "G":
            prepare(op[1])
        elif op[0] == "g":
            g, j = op[1:]
            n = 1
            while n < 2 and PLAN[at] == ("g", g, j + n):
                at, n = at + 1, n + 1
            chunk(g, j, n, g not in seen)
            seen.add(g)
        elif op[0] == "F":
            finish(op[1], finished == 0)
            finished += 1
        elif op[0] == "R":
            pass_on(*op[1:])
        elif op[0] in ("r", "wr"):
            row_step(op)
        else:
            col_step(op)

    size = hid // (4 * NZ)
    for hi in range(2):
        for zz in range(NZ):
            for core in range(2):
                start = ((hi * NZ + zz) * 2 + core) * size
                pbuf[hi, core, zz] = (terms[start : start + size, :] * final).astype(BF)
    zs = pl.ds(k * (NZ // 2), NZ // 2)
    others = pl.ds((1 - k) * (NZ // 2), NZ // 2)
    send(pbuf.at[:, :, others], xrec, (pair_send, 0), pair_recv.at[0], partner)
    arrived(xrec, pair_recv.at[0])
    both = pbuf[:, :, zs].astype(F32) + xrec[...].astype(F32)
    pbuf[:, :, zs] = both.astype(BF)

    def portion(xx, yy):
        return yy // 2, yy % 2, zs, slice(None), pl.ds(pl.multiple_of(xx * 128, 128), 128)

    for dx in range(NX):
        for dy in range(NY):
            if dx or dy:
                to = ((NX - dx) % NX, (NY - dy) % NY)
                send(
                    pbuf.at[portion((x + dx) % NX, (y + dy) % NY)],
                    prec.at[to[0], to[1]],
                    (p_send, dx, dy),
                    p_recv.at[to[0], to[1]],
                    dev(dx, dy, 0),
                )

    for op in PLAN[at:]:
        pass_on(*op[1:])
    for i in range(PARTS):
        ps = pl.ds(i * piece, piece)
        arrived(rplus.at[3, ps, :], rs_recv.at[0, 3, i])
        arrived(rminus.at[3, ps, :], rs_recv.at[1, 3, i])
    total = moved[0:pts, :] + rplus[3].astype(F32) + rminus[3].astype(F32)
    grad = (total * final).astype(BF)
    gh_ref[...] = lax.dot_general(grad, proj_ref[...], NT, preferred_element_type=F32).astype(BF)

    share = pbuf[portion(x, y)].astype(F32)
    for dx in range(NX):
        for dy in range(NY):
            if dx or dy:
                arrived(prec.at[dx, dy], p_recv.at[dx, dy])
                share = share + prec[dx, dy].astype(F32)
    zbuf[...] = share.astype(BF)

    gathers = k == z // (NZ // 2)
    later = []

    def send_if(cond, src, dst, send_sem, recv_sem, to):
        copy = pltpu.make_async_remote_copy(
            src_ref=src,
            dst_ref=dst,
            send_sem=send_sem,
            recv_sem=recv_sem,
            device_id=to,
            device_id_type=MESH,
        )

        @pl.when(cond)
        def _():
            copy.start()

        later.append((cond, copy))

    for dz in range(1, NZ):
        zz = (z + dz) % NZ
        send_if(
            zz // (NZ // 2) == k,
            zbuf.at[zz % (NZ // 2)],
            zrec.at[NZ - dz],
            z_send.at[dz],
            z_recv.at[NZ - dz],
            dev(0, 0, dz),
        )

    @pl.when(gathers)
    def _():
        total = zbuf[z % (NZ // 2)].astype(F32)
        for dz in range(1, NZ):
            arrived(zrec.at[dz], z_recv.at[dz])
            total = total + zrec[dz].astype(F32)
        fbuf[...] = total

    mine = y_lo == k
    for dx in range(NX):
        for flip in range(2):
            xx, yy = (x + dx) % NX, y_hi * 2 + (y_lo if flip == 0 else 1 - y_lo)
            to = ((y_hi * NZ + z) * 2 + y_lo, xx * 2 + yy % 2)
            cond = gathers if dx or flip else gathers & jnp.logical_not(mine)
            slot = (NX - dx) % NX
            send_if(cond, fbuf, frec.at[slot], f_send.at[dx, flip], f_recv.at[slot], to)

    @pl.when(gathers & mine)
    def _():
        frec[0] = fbuf[...]

    for dx in range(NX):
        if dx == 0:

            @pl.when(jnp.logical_not(gathers & mine))
            def _():
                arrived(frec.at[0], f_recv.at[0])

        else:
            arrived(frec.at[dx], f_recv.at[dx])
        gp_ref[:, pl.ds(pl.multiple_of((x + dx) % NX * 128, 128), 128)] = frec[dx]

    for copy in sends:
        copy.wait_send()
    for cond, copy in later:

        @pl.when(cond)
        def _():
            copy.wait_send()


def fused(hidden, projection, alpha, probe_pairs, amplitude, length_sq):
    pts, hid = hidden.shape
    feat = projection.shape[1]
    probes = probe_pairs.shape[1] // 2
    width = feat + AUX
    n_rows, n_cols = NZ * pts, 2 * NX * NY * pts
    size = hid // (4 * NZ)
    vmem = pl.BlockSpec(memory_space=pltpu.VMEM)
    smem = pl.BlockSpec(memory_space=pltpu.SMEM)
    dma = pltpu.SemaphoreType.DMA
    return pl.pallas_call(
        functools.partial(kernel, probes),
        out_shape=(
            jax.ShapeDtypeStruct((pts, hid), BF),
            jax.ShapeDtypeStruct((hid // (4 * NZ), feat), F32),
        ),
        in_specs=[smem, smem, vmem, vmem, vmem, vmem],
        out_specs=(vmem, vmem),
        scratch_shapes=[
            pltpu.VMEM((n_rows, hid + AUX), BF),
            pltpu.VMEM((n_rows, feat), BF),
            pltpu.VMEM((n_cols, width), BF),
            pltpu.VMEM((n_rows, AUX), BF),
            pltpu.VMEM((n_rows, 1), F32),
            pltpu.VMEM((n_rows, feat), F32),
            pltpu.VMEM((n_rows, 128), F32),
            pltpu.VMEM((n_rows, feat), BF),
            pltpu.VMEM((4, pts, feat), BF),
            pltpu.VMEM((4, pts, feat), BF),
            pltpu.VMEM((hid, feat), F32),
            pltpu.VMEM((2, 2, NZ, size, feat), BF),
            pltpu.VMEM((2, 2, NZ // 2, size, feat), BF),
            pltpu.VMEM((NX, NY, NZ // 2, size, 128), BF),
            pltpu.VMEM((NZ // 2, size, 128), BF),
            pltpu.VMEM((NZ, size, 128), BF),
            pltpu.VMEM((size, 128), F32),
            pltpu.VMEM((NX, size, 128), F32),
            dma((28,)),
            dma((NZ, 4)),
            dma((60,)),
            dma((NX, NY, 4)),
            dma((32,)),
            dma((NX, NY, 2)),
            dma((7 * PARTS,)),
            dma((2, 4, PARTS)),
            dma((1,)),
            dma((1,)),
            dma((NX, NY)),
            dma((NX, NY)),
            dma((NZ,)),
            dma((NZ,)),
            dma((NX, 2)),
            dma((NX,)),
        ],
        compiler_params=pltpu.CompilerParams(
            collective_id=0, has_side_effects=True, vmem_limit_bytes=56 << 20
        ),
        name="fused",
    )(amplitude, length_sq, hidden, projection, alpha[None, :], probe_pairs.T)


def per_device(hidden, projection, alpha, probe_pairs, amplitude, length_sq):
    return fused(hidden, projection, alpha, probe_pairs, amplitude, length_sq)


def solution(mesh):
    placed = (P(("row", "col"), None), P(), P(("row", "col")), P(("row", "col"), None), P(), P())
    return jax.shard_map(
        per_device,
        mesh=mesh,
        in_specs=placed,
        out_specs=(P(("row", "col"), None), P("row", None)),
        check_vma=False,
    )
```

time: 78.1 us -> 68.9 us (0.88)
  Pallas kernels: 73.7 us -> 64.6 us
    pallas_call x1, Pallas kernels: 73.7 us -> 64.6 us  [fused(): pl.pallas_call(functools.partial(kernel, probes), out_shape=(jax.ShapeDty...]
where the time goes in v3:
time: 68.9 us; the launch traced here: 68.8 us
  Pallas kernels  64.6 us (94%)
  local copies, waits for them, and re-layouts  2.25 us (3%)
  between operations  1.94 us (3%)
    pallas_call x1, Pallas kernels, fused(): pl.pallas_call(functools.partial(kernel, probes), out_shape=(jax.ShapeDty...  64.6 us
    unnamed x4, local copies, waits for them, and re-layouts  2.25 us

profile of v3, /device:TPU:1, one launch (start us, length us, event | category | flops | bytes accessed | tf_op | source)
XLA Modules:
  0.0 68.8 jit_solution(3801873130341907264)
XLA Ops:
  1.9 64.6 %fused.1 = (bf16[128,768]{1,0:T(8,128)(2,1)}, f32[24,512]{1,0:T(8,128)}) custom-call(f32[1]{0:T(128)S(6)} %copy.10.amp_ref, f32[1]{0:T(128)S(6)} %copy.11.lsq_ref, bf16[128,768]{1,0:T(8,128)(2,1)} %hidden_ref.1, bf16[768,512]{1,0:T(8,128)(2,1)} %proj_ref.1, bf16[1,128]{1,0:T(2,128)(2,1)} %bitcast.3, bf16[32,128]{1,0:T(8,128)(2,1)} %bitcast.2), custom_call_target="tpu_custom_call" | custom-call | tf_op jit(solution)/shard_map/fused/pallas_call | solution.py:458
  66.5 0.0 copy-start
  66.5 1.6 %copy.12 = bf16[128,768]{1,0:T(8,128)(2,1)} copy(bf16[128,768]{1,0:T(8,128)(2,1)} %get-tuple-element.4) | data formatting | bytes 393216
  68.1 0.0 copy-done
  68.1 0.6 copy.13
Async XLA Ops:
  66.5 1.6 %copy-start = (f32[24,512]{1,0:T(8,128)S(1)}, f32[24,512]{1,0:T(8,128)}, u32[]{:S(2)}) copy-start(f32[24,512]{1,0:T(8,128)} %get-tuple-element.5) | copy-start | bytes 147460

commit v4 on v3

--- a/solution.py
+++ b/solution.py
@@ -31,51 +31,50 @@
     ("c", 0, 0, 3, 0, 1, 2), ("c", 0, 0, 0, 3, 0, 1), ("c", 0, 0, 1, 3, 0, 1), ("c", 0, 0, 2, 0, 3, 3),
     ("c", 0, 0, 3, 0, 3, 3), ("c", 0, 0, 0, 0, 1, 2), ("c", 0, 0, 1, 0, 1, 2), ("c", 0, 0, 2, 1, 0, 0),
     ("c", 0, 0, 3, 1, 0, 0), ("c", 0, 0, 0, 0, 3, 3), ("c", 0, 0, 1, 0, 3, 3), ("c", 0, 0, 2, 3, 0, 1),
-    ("c", 0, 0, 3, 3, 0, 1), ("p", 0, 0, 0), ("p", 0, 0, 1), ("wp", 0, 0, 0), ("wp", 0, 0, 1), ("wc", 0, 1, 2),
-    ("c", 0, 1, 2, 0, 2, 2), ("c", 0, 1, 2, 1, 1, 0), ("c", 0, 1, 2, 3, 1, 1), ("wc", 0, 3, 2),
-    ("c", 0, 3, 2, 1, 3, 0), ("c", 0, 3, 2, 3, 3, 1), ("wc", 1, 0, 0), ("c", 1, 0, 0, 2, 0, 0),
-    ("c", 1, 0, 0, 1, 1, 2), ("c", 1, 0, 0, 1, 3, 3), ("wc", 3, 0, 0), ("c", 3, 0, 0, 3, 1, 2),
-    ("c", 3, 0, 0, 3, 3, 3), ("wr", 1, 0), ("r", 1, 0, 2, 0), ("wr", 7, 0), ("r", 7, 0, 6, 1), ("wc", 0, 1, 3),
+    ("c", 0, 0, 3, 3, 0, 1), ("p", 0, 0, 0), ("p", 0, 0, 1), ("wp", 0, 0, 0), ("wp", 0, 0, 1), ("wr", 1, 0),
+    ("r", 1, 0, 2, 0), ("wr", 7, 0), ("r", 7, 0, 6, 1), ("wc", 0, 1, 2), ("c", 0, 1, 2, 0, 2, 2),
+    ("c", 0, 1, 2, 1, 1, 0), ("c", 0, 1, 2, 3, 1, 1), ("wc", 0, 3, 2), ("c", 0, 3, 2, 1, 3, 0),
+    ("c", 0, 3, 2, 3, 3, 1), ("wc", 1, 0, 0), ("c", 1, 0, 0, 2, 0, 0), ("c", 1, 0, 0, 1, 1, 2),
+    ("c", 1, 0, 0, 1, 3, 3), ("wc", 3, 0, 0), ("c", 3, 0, 0, 3, 1, 2), ("c", 3, 0, 0, 3, 3, 3), ("wc", 0, 1, 3),
     ("c", 0, 1, 3, 1, 1, 0), ("c", 0, 1, 3, 3, 1, 1), ("p", 0, 1, 1), ("wc", 0, 3, 3), ("c", 0, 3, 3, 0, 2, 3),
     ("c", 0, 3, 3, 1, 3, 0), ("c", 0, 3, 3, 3, 3, 1), ("p", 0, 3, 1), ("wc", 1, 0, 1), ("c", 1, 0, 1, 1, 1, 2),
     ("c", 1, 0, 1, 1, 3, 3), ("p", 1, 0, 0), ("wc", 3, 0, 1), ("c", 3, 0, 1, 2, 0, 1), ("c", 3, 0, 1, 3, 1, 2),
     ("c", 3, 0, 1, 3, 3, 3), ("p", 3, 0, 0), ("wr", 1, 1), ("r", 1, 1, 2, 0), ("wr", 7, 1), ("r", 7, 1, 6, 1),
     ("wc", 0, 1, 0), ("c", 0, 1, 0, 0, 2, 2), ("wc", 0, 3, 0), ("wc", 1, 0, 2), ("c", 1, 0, 2, 2, 0, 0),
-    ("wc", 3, 0, 2), ("wp", 0, 1, 1), ("wp", 0, 3, 1), ("wc", 0, 1, 1), ("p", 0, 1, 0), ("wc", 0, 3, 1),
-    ("c", 0, 3, 1, 0, 2, 3), ("p", 0, 3, 0), ("wc", 1, 0, 3), ("p", 1, 0, 1), ("wc", 3, 0, 3),
-    ("c", 3, 0, 3, 2, 0, 1), ("p", 3, 0, 1), ("wp", 1, 0, 0), ("wr", 1, 2), ("r", 1, 2, 2, 0), ("wr", 7, 2),
-    ("r", 7, 2, 6, 1), ("wp", 3, 0, 0), ("wc", 0, 2, 2), ("c", 0, 2, 2, 1, 2, 0), ("c", 0, 2, 2, 3, 2, 1),
-    ("wc", 1, 1, 2), ("c", 1, 1, 2, 2, 1, 0), ("wc", 1, 3, 0), ("wc", 3, 1, 2), ("wp", 0, 1, 0), ("wr", 1, 3),
-    ("r", 1, 3, 2, 0), ("wr", 7, 3), ("r", 7, 3, 6, 1), ("wp", 0, 3, 0), ("G", 3), ("g", 3, 0), ("wr", 2, 0),
-    ("r", 2, 0, 3, 0), ("wr", 6, 0), ("r", 6, 0, 5, 1), ("wc", 0, 2, 3), ("c", 0, 2, 3, 1, 2, 0),
-    ("c", 0, 2, 3, 3, 2, 1), ("p", 0, 2, 1), ("wc", 2, 0, 0), ("c", 2, 0, 0, 2, 1, 2), ("c", 2, 0, 0, 2, 3, 3),
-    ("wc", 1, 1, 0), ("c", 1, 1, 0, 1, 2, 2), ("wc", 1, 3, 2), ("c", 1, 3, 2, 2, 3, 0), ("wc", 3, 3, 0),
-    ("wc", 3, 3, 2), ("wc", 3, 1, 0), ("c", 3, 1, 0, 3, 2, 2), ("wc", 3, 1, 3), ("c", 3, 1, 3, 2, 1, 1),
-    ("p", 3, 1, 1), ("wp", 1, 0, 1), ("wc", 1, 1, 1), ("p", 1, 1, 0), ("wc", 1, 1, 3), ("p", 1, 1, 1),
-    ("wc", 1, 3, 1), ("c", 1, 3, 1, 1, 2, 3), ("p", 1, 3, 0), ("wc", 3, 3, 3), ("c", 3, 3, 3, 2, 3, 1),
-    ("p", 3, 3, 1), ("wp", 3, 0, 1), ("wr", 2, 1), ("r", 2, 1, 3, 0), ("wr", 6, 1), ("r", 6, 1, 5, 1),
-    ("wc", 2, 0, 1), ("c", 2, 0, 1, 2, 1, 2), ("c", 2, 0, 1, 2, 3, 3), ("p", 2, 0, 0), ("wc", 1, 3, 3),
-    ("p", 1, 3, 1), ("wc", 3, 1, 1), ("p", 3, 1, 0), ("wc", 3, 3, 1), ("c", 3, 3, 1, 3, 2, 3), ("p", 3, 3, 0),
-    ("wp", 0, 2, 1), ("wp", 3, 1, 1), ("wr", 2, 2), ("r", 2, 2, 3, 0), ("wr", 6, 2), ("r", 6, 2, 5, 1),
-    ("wp", 1, 1, 0), ("wc", 0, 2, 0), ("wc", 0, 2, 1), ("p", 0, 2, 0), ("wc", 2, 0, 2), ("wc", 2, 0, 3),
-    ("p", 2, 0, 1), ("wp", 1, 1, 1), ("g", 3, 1), ("wr", 2, 3), ("r", 2, 3, 3, 0), ("wr", 6, 3), ("r", 6, 3, 5, 1),
-    ("wc", 1, 2, 2), ("c", 1, 2, 2, 2, 2, 0), ("wc", 3, 2, 2), ("wc", 2, 1, 0), ("c", 2, 1, 0, 2, 2, 2),
-    ("wc", 2, 3, 0), ("wp", 1, 3, 0), ("wp", 3, 3, 1), ("wp", 2, 0, 0), ("wp", 1, 3, 1), ("wp", 3, 1, 0), ("G", 2),
-    ("g", 2, 0), ("wr", 3, 0), ("r", 3, 0, 4, 0), ("wr", 5, 0), ("wc", 3, 2, 3), ("c", 3, 2, 3, 2, 2, 1),
-    ("p", 3, 2, 1), ("wc", 1, 2, 3), ("p", 1, 2, 1), ("wc", 2, 3, 1), ("c", 2, 3, 1, 2, 2, 3), ("p", 2, 3, 0),
-    ("wc", 2, 1, 2), ("wr", 3, 1), ("r", 3, 1, 4, 0), ("wr", 5, 1), ("wc", 1, 2, 0), ("wc", 1, 2, 1), ("p", 1, 2, 0),
-    ("wc", 2, 1, 3), ("p", 2, 1, 1), ("wc", 3, 2, 0), ("wc", 2, 3, 2), ("wc", 2, 3, 3), ("p", 2, 3, 1),
-    ("wp", 3, 3, 0), ("wp", 0, 2, 0), ("wp", 2, 0, 1), ("g", 2, 1), ("wr", 3, 2), ("wr", 5, 2), ("r", 5, 2, 4, 1),
-    ("wc", 2, 1, 1), ("p", 2, 1, 0), ("wc", 3, 2, 1), ("p", 3, 2, 0), ("wc", 2, 2, 2), ("wc", 2, 2, 0),
-    ("wp", 3, 2, 1), ("wp", 1, 2, 1), ("g", 2, 2), ("wr", 3, 3), ("wr", 5, 3), ("r", 5, 3, 4, 1), ("wp", 2, 3, 0),
-    ("wp", 1, 2, 0), ("wp", 2, 1, 1), ("wp", 2, 3, 1), ("wp", 2, 1, 0), ("G", 1), ("g", 1, 0), ("wr", 4, 0),
-    ("wc", 2, 2, 3), ("p", 2, 2, 1), ("wc", 2, 2, 1), ("p", 2, 2, 0), ("wp", 3, 2, 0), ("g", 1, 1), ("wr", 4, 1),
-    ("wr", 4, 2), ("wp", 2, 2, 1), ("g", 1, 2), ("wr", 4, 3), ("wp", 2, 2, 0), ("G", 0), ("g", 0, 0), ("g", 0, 1),
-    ("g", 0, 2), ("g", 0, 3), ("F", 0), ("R", 4, 0), ("R", 4, 1), ("R", 4, 2), ("R", 4, 3), ("g", 1, 3), ("F", 1),
-    ("R", 3, 2), ("R", 3, 3), ("R", 5, 0), ("R", 5, 1), ("g", 2, 3), ("F", 2), ("R", 3, 0), ("R", 3, 1), ("R", 5, 2),
-    ("R", 5, 3), ("g", 3, 2), ("R", 2, 2), ("R", 2, 3), ("R", 6, 0), ("R", 6, 1), ("g", 3, 3), ("F", 3), ("R", 2, 0),
-    ("R", 2, 1), ("R", 6, 2), ("R", 6, 3), ("R", 1, 2), ("R", 7, 0), ("R", 1, 3), ("R", 7, 1), ("R", 1, 0),
-    ("R", 7, 2), ("R", 1, 1), ("R", 7, 3),
+    ("wc", 3, 0, 2), ("wp", 0, 1, 1), ("wr", 1, 2), ("r", 1, 2, 2, 0), ("wr", 7, 2), ("r", 7, 2, 6, 1),
+    ("wp", 0, 3, 1), ("wc", 0, 1, 1), ("p", 0, 1, 0), ("wc", 0, 3, 1), ("c", 0, 3, 1, 0, 2, 3), ("p", 0, 3, 0),
+    ("wc", 1, 0, 3), ("p", 1, 0, 1), ("wc", 3, 0, 3), ("c", 3, 0, 3, 2, 0, 1), ("p", 3, 0, 1), ("wp", 1, 0, 0),
+    ("wp", 3, 0, 0), ("wr", 1, 3), ("r", 1, 3, 2, 0), ("wr", 7, 3), ("r", 7, 3, 6, 1), ("wc", 0, 2, 2),
+    ("c", 0, 2, 2, 1, 2, 0), ("c", 0, 2, 2, 3, 2, 1), ("wc", 1, 1, 2), ("c", 1, 1, 2, 2, 1, 0), ("wc", 1, 3, 0),
+    ("wc", 3, 1, 2), ("wp", 0, 1, 0), ("wp", 0, 3, 0), ("G", 3), ("g", 3, 0), ("wr", 2, 0), ("r", 2, 0, 3, 0),
+    ("wr", 6, 0), ("r", 6, 0, 5, 1), ("wc", 0, 2, 3), ("c", 0, 2, 3, 1, 2, 0), ("c", 0, 2, 3, 3, 2, 1),
+    ("p", 0, 2, 1), ("wc", 2, 0, 0), ("c", 2, 0, 0, 2, 1, 2), ("c", 2, 0, 0, 2, 3, 3), ("wc", 1, 1, 0),
+    ("c", 1, 1, 0, 1, 2, 2), ("wc", 1, 3, 2), ("c", 1, 3, 2, 2, 3, 0), ("wc", 3, 3, 0), ("wc", 3, 3, 2),
+    ("wc", 3, 1, 0), ("c", 3, 1, 0, 3, 2, 2), ("wc", 3, 1, 3), ("c", 3, 1, 3, 2, 1, 1), ("p", 3, 1, 1),
+    ("wp", 1, 0, 1), ("wp", 3, 0, 1), ("wr", 2, 1), ("r", 2, 1, 3, 0), ("wr", 6, 1), ("r", 6, 1, 5, 1),
+    ("wc", 1, 1, 1), ("p", 1, 1, 0), ("wc", 1, 1, 3), ("p", 1, 1, 1), ("wc", 1, 3, 1), ("c", 1, 3, 1, 1, 2, 3),
+    ("p", 1, 3, 0), ("wc", 3, 3, 3), ("c", 3, 3, 3, 2, 3, 1), ("p", 3, 3, 1), ("wp", 0, 2, 1), ("wc", 2, 0, 1),
+    ("c", 2, 0, 1, 2, 1, 2), ("c", 2, 0, 1, 2, 3, 3), ("p", 2, 0, 0), ("wc", 1, 3, 3), ("p", 1, 3, 1),
+    ("wc", 3, 1, 1), ("p", 3, 1, 0), ("wc", 3, 3, 1), ("c", 3, 3, 1, 3, 2, 3), ("p", 3, 3, 0), ("wp", 3, 1, 1),
+    ("wr", 2, 2), ("r", 2, 2, 3, 0), ("wr", 6, 2), ("r", 6, 2, 5, 1), ("wp", 1, 1, 0), ("wp", 1, 1, 1),
+    ("wc", 0, 2, 0), ("wc", 0, 2, 1), ("p", 0, 2, 0), ("wc", 2, 0, 2), ("wc", 2, 0, 3), ("p", 2, 0, 1), ("g", 3, 1),
+    ("wr", 2, 3), ("r", 2, 3, 3, 0), ("wr", 6, 3), ("r", 6, 3, 5, 1), ("wc", 1, 2, 2), ("c", 1, 2, 2, 2, 2, 0),
+    ("wc", 3, 2, 2), ("wp", 1, 3, 0), ("wc", 2, 1, 0), ("c", 2, 1, 0, 2, 2, 2), ("wc", 2, 3, 0), ("wp", 3, 3, 1),
+    ("wp", 2, 0, 0), ("wp", 1, 3, 1), ("G", 2), ("g", 2, 0), ("wr", 3, 0), ("r", 3, 0, 4, 0), ("wr", 5, 0),
+    ("wc", 3, 2, 3), ("c", 3, 2, 3, 2, 2, 1), ("p", 3, 2, 1), ("wc", 2, 1, 2), ("wc", 1, 2, 0), ("wc", 1, 2, 1),
+    ("p", 1, 2, 0), ("wp", 3, 1, 0), ("wp", 3, 3, 0), ("wp", 0, 2, 0), ("wp", 2, 0, 1), ("g", 2, 1), ("wr", 3, 1),
+    ("r", 3, 1, 4, 0), ("wr", 5, 1), ("wc", 1, 2, 3), ("p", 1, 2, 1), ("wc", 2, 3, 1), ("c", 2, 3, 1, 2, 2, 3),
+    ("p", 2, 3, 0), ("wc", 2, 1, 3), ("p", 2, 1, 1), ("wc", 3, 2, 0), ("wc", 2, 3, 2), ("wc", 2, 3, 3),
+    ("p", 2, 3, 1), ("wc", 2, 1, 1), ("p", 2, 1, 0), ("wc", 3, 2, 1), ("p", 3, 2, 0), ("g", 2, 2), ("wr", 3, 2),
+    ("wr", 5, 2), ("r", 5, 2, 4, 1), ("wc", 2, 2, 2), ("wc", 2, 2, 0), ("wp", 3, 2, 1), ("wp", 1, 2, 0), ("g", 3, 2),
+    ("wr", 3, 3), ("wr", 5, 3), ("r", 5, 3, 4, 1), ("wp", 1, 2, 1), ("wp", 2, 3, 0), ("wp", 2, 1, 1), ("wp", 2, 3, 1),
+    ("G", 1), ("g", 1, 0), ("wr", 4, 0), ("wc", 2, 2, 3), ("p", 2, 2, 1), ("wc", 2, 2, 1), ("p", 2, 2, 0),
+    ("wp", 2, 1, 0), ("wp", 3, 2, 0), ("g", 1, 1), ("wr", 4, 1), ("g", 1, 2), ("wr", 4, 2), ("wp", 2, 2, 1),
+    ("wp", 2, 2, 0), ("g", 1, 3), ("F", 1), ("wr", 4, 3), ("R", 3, 2), ("R", 3, 3), ("R", 5, 0), ("R", 5, 1),
+    ("G", 0), ("g", 0, 0), ("g", 0, 1), ("g", 0, 2), ("g", 0, 3), ("F", 0), ("R", 4, 0), ("R", 4, 1), ("R", 4, 2),
+    ("R", 4, 3), ("g", 2, 3), ("F", 2), ("R", 2, 2), ("R", 2, 3), ("R", 6, 0), ("R", 6, 1), ("g", 3, 3), ("F", 3),
+    ("R", 3, 0), ("R", 5, 2), ("R", 3, 1), ("R", 5, 3), ("R", 1, 2), ("R", 7, 0), ("R", 1, 3), ("R", 7, 1),
+    ("R", 2, 0), ("R", 6, 2), ("R", 2, 1), ("R", 6, 3), ("R", 1, 0), ("R", 7, 2), ("R", 1, 1), ("R", 7, 3),
 ]
 
 
@@ -83,8 +82,8 @@
     return lax.broadcasted_iota(jnp.int32, shape, dim)
 
 
-def aux_block(feats, alpha_row, probe_t, probes):
-    points = feats.shape[0]
+def factor_block(alpha_row, probe_t, probes):
+    points = alpha_row.shape[1]
     src, lane = iota((2 * probes, AUX), 0), iota((2 * probes, AUX), 1)
     scale = 1.0 / (4 * probes)
     swapped = jnp.where(src < probes, src + probes, src - probes)
@@ -95,23 +94,31 @@
     lane = iota((points, AUX), 1)
     put = jnp.where(lane == 2 * probes, 1.0, 0.0) + jnp.where(lane == 64 + 2 * probes, 0.5, 0.0)
     aux = aux + jnp.dot(diag.astype(BF), put.astype(BF), preferred_element_type=F32)
+    return aux
+
+
+def norms_of(feats):
     f = feats.astype(F32)
-    rest = jnp.sum(f * f, axis=1, keepdims=True)
+    return jnp.sum(f * f, axis=1, keepdims=True)
+
+
+def with_norms(factors, norms):
+    lane = iota(factors.shape, 1)
     for k in range(3):
-        part = rest.astype(BF).astype(F32)
-        aux = jnp.where(lane == 100 + k, part, aux)
-        rest = rest - part
-    return aux
+        part = norms.astype(BF).astype(F32)
+        factors = jnp.where(lane == 100 + k, part, factors)
+        norms = norms - part
+    return factors
 
 
 def kernel(
     probes,
     amp_ref,
     lsq_ref,
-    hidden_ref,
-    proj_ref,
-    alpha_ref,
-    probe_ref,
+    hidden_hbm,
+    proj_hbm,
+    alpha_hbm,
+    probe_hbm,
     gh_ref,
     gp_ref,
     rows,
@@ -148,8 +155,12 @@
     z_recv,
     f_send,
     f_recv,
+    proj_ref,
+    alpha_ref,
+    probe_ref,
+    in_sem,
 ):
-    pts, hid = hidden_ref.shape
+    pts, hid = hidden_hbm.shape
     feat = proj_ref.shape[1]
     width = feat + AUX
     half, quarter, piece = pts // 2, pts // 4, pts // PARTS
@@ -169,18 +180,31 @@
     line = (dev(0, 0, -1), dev(0, 0, 1))
     partner = dev(0, 0, 0, 1)
 
+    own_rows = pl.ds(POS[0] * pts, pts)
+    hidden_ref = rows.at[own_rows, pl.ds(0, hid)]
+    loads = [
+        pltpu.make_async_copy(src, dst, in_sem.at[i])
+        for i, (src, dst) in enumerate(
+            (
+                (hidden_hbm, hidden_ref),
+                (alpha_hbm, alpha_ref),
+                (probe_hbm, probe_ref),
+                (proj_hbm, proj_ref),
+            )
+        )
+    ]
+    for load in loads:
+        load.start()
+
     barrier = pltpu.get_barrier_semaphore()
     for peer in (*plane, *line, partner):
         pl.semaphore_signal(barrier, inc=1, device_id=peer, device_id_type=MESH)
 
-    feats = jnp.dot(hidden_ref[...], proj_ref[...], preferred_element_type=F32).astype(BF)
-    aux = aux_block(feats, alpha_ref[...], probe_ref[...], probes).astype(BF)
-    own = pl.ds(SLOTS.index((0, 0, 0)) * pts, pts)
-    cols[own, 0:feat] = feats
-    cols[own, feat:width] = aux
-    own = pl.ds(POS[0] * pts, pts)
-    rows[own, 0:hid] = hidden_ref[...]
-    rows[own, hid : hid + AUX] = aux
+    for load in loads[1:3]:
+        load.wait()
+    factors = factor_block(alpha_ref[...], probe_ref[...], probes)
+    rows[own_rows, hid : hid + AUX] = factors.astype(BF)
+    loads[0].wait()
 
     pl.semaphore_wait(barrier, 7)
 
@@ -228,13 +252,11 @@
 
     def prepare(g):
         rs = pl.ds(g * m, m)
-        row_feat[rs, :] = jnp.dot(
-            rows[rs, 0:hid], proj_ref[...], preferred_element_type=F32
-        ).astype(BF)
+        feats = jnp.dot(rows[rs, 0:hid], proj_ref[...], preferred_element_type=F32).astype(BF)
+        row_feat[rs, :] = feats
+        bias[rs, :] = norms_of(feats) * (-0.5 * scale)
         lane = iota((m, AUX), 1)
         raw = rows[rs, hid : hid + AUX].astype(F32)
-        norms = jnp.where((lane >= 100) & (lane < 103), raw, 0.0)
-        bias[rs, :] = jnp.sum(norms, axis=1, keepdims=True) * (-0.5 * scale)
         turned = pltpu.roll(raw, 64, 1)
         factors = jnp.where((lane >= 64) & (lane <= 64 + 2 * probes), turned, 0.0)
         left[rs, :] = factors.astype(BF)
@@ -304,8 +326,17 @@
                 src = col_part(0, dx, dy, 2 * h, 2)
                 send(src, dst, part_send, part_recv.at[dx, dy, h], partner)
 
+    at = 0
+    while PLAN[at][0] == "r":
+        row_step(PLAN[at])
+        at += 1
+    loads[3].wait()
+    feats = jnp.dot(hidden_ref[...], proj_ref[...], preferred_element_type=F32).astype(BF)
+    own = pl.ds(SLOTS.index((0, 0, 0)) * pts, pts)
+    cols[own, 0:feat] = feats
+    cols[own, feat:width] = with_norms(factors, norms_of(feats)).astype(BF)
+
     seen, finished = set(), 0
-    at = 0
     while finished < GROUPS:
         op = PLAN[at]
         at += 1
@@ -328,21 +359,14 @@
         else:
             col_step(op)
 
-    size = hid // (4 * NZ)
-    for hi in range(2):
-        for zz in range(NZ):
-            for core in range(2):
-                start = ((hi * NZ + zz) * 2 + core) * size
-                pbuf[hi, core, zz] = (terms[start : start + size, :] * final).astype(BF)
-    zs = pl.ds(k * (NZ // 2), NZ // 2)
-    others = pl.ds((1 - k) * (NZ // 2), NZ // 2)
-    send(pbuf.at[:, :, others], xrec, (pair_send, 0), pair_recv.at[0], partner)
+    pbuf[...] = (terms[...] * final).astype(BF).reshape(pbuf.shape)
+    send(pbuf.at[:, :, 1 - k], xrec, (pair_send, 0), pair_recv.at[0], partner)
     arrived(xrec, pair_recv.at[0])
-    both = pbuf[:, :, zs].astype(F32) + xrec[...].astype(F32)
-    pbuf[:, :, zs] = both.astype(BF)
+    pbuf[:, :, k] = (pbuf[:, :, k].astype(F32) + xrec[...].astype(F32)).astype(BF)
 
     def portion(xx, yy):
-        return yy // 2, yy % 2, zs, slice(None), pl.ds(pl.multiple_of(xx * 128, 128), 128)
+        lanes = pl.ds(pl.multiple_of(xx * 128, 128), 128)
+        return yy // 2, yy % 2, k, slice(None), slice(None), lanes
 
     for dx in range(NX):
         for dy in range(NY):
@@ -374,7 +398,10 @@
                 share = share + prec[dx, dy].astype(F32)
     zbuf[...] = share.astype(BF)
 
-    gathers = k == z // (NZ // 2)
+    def falls_here(zz):
+        return (zz // 4 == y_lo) & (zz % 4 // 2 == k)
+
+    gathers = falls_here(z)
     later = []
 
     def send_if(cond, src, dst, send_sem, recv_sem, to):
@@ -393,11 +420,11 @@
 
         later.append((cond, copy))
 
-    for dz in range(1, NZ):
+    for dz in (4, 3, 5, 2, 6, 1, 7):
         zz = (z + dz) % NZ
         send_if(
-            zz // (NZ // 2) == k,
-            zbuf.at[zz % (NZ // 2)],
+            falls_here(zz),
+            zbuf.at[zz % 2],
             zrec.at[NZ - dz],
             z_send.at[dz],
             z_recv.at[NZ - dz],
@@ -406,35 +433,41 @@
 
     @pl.when(gathers)
     def _():
-        total = zbuf[z % (NZ // 2)].astype(F32)
+        total = zbuf[z % 2].astype(F32)
         for dz in range(1, NZ):
             arrived(zrec.at[dz], z_recv.at[dz])
             total = total + zrec[dz].astype(F32)
-        fbuf[...] = total
-
-    mine = y_lo == k
-    for dx in range(NX):
-        for flip in range(2):
-            xx, yy = (x + dx) % NX, y_hi * 2 + (y_lo if flip == 0 else 1 - y_lo)
-            to = ((y_hi * NZ + z) * 2 + y_lo, xx * 2 + yy % 2)
-            cond = gathers if dx or flip else gathers & jnp.logical_not(mine)
-            slot = (NX - dx) % NX
-            send_if(cond, fbuf, frec.at[slot], f_send.at[dx, flip], f_recv.at[slot], to)
-
-    @pl.when(gathers & mine)
+        fbuf[...] = total.reshape(fbuf.shape).astype(BF)
+
+    for flip in (1, 0):
+        for dx in (2, 1, 3, 0):
+            for core in range(2):
+                xx, yy = (x + dx) % NX, (y_lo if flip == 0 else 1 - y_lo)
+                to = ((y_hi * NZ + z) * 2 + core, xx * 2 + yy)
+                slot = (NX - dx) % NX
+                send_if(
+                    gathers if dx or flip else gathers & (k != core),
+                    fbuf.at[core],
+                    frec.at[slot],
+                    f_send.at[dx, flip, core],
+                    f_recv.at[slot],
+                    to,
+                )
+
+    @pl.when(gathers)
     def _():
-        frec[0] = fbuf[...]
+        frec[0] = fbuf[k]
 
     for dx in range(NX):
         if dx == 0:
 
-            @pl.when(jnp.logical_not(gathers & mine))
+            @pl.when(jnp.logical_not(gathers))
             def _():
                 arrived(frec.at[0], f_recv.at[0])
 
         else:
             arrived(frec.at[dx], f_recv.at[dx])
-        gp_ref[:, pl.ds(pl.multiple_of((x + dx) % NX * 128, 128), 128)] = frec[dx]
+        gp_ref[:, pl.ds(pl.multiple_of((x + dx) % NX * 128, 128), 128)] = frec[dx].astype(F32)
 
     for copy in sends:
         copy.wait_send()
@@ -453,6 +486,7 @@
     n_rows, n_cols = NZ * pts, 2 * NX * NY * pts
     size = hid // (4 * NZ)
     vmem = pl.BlockSpec(memory_space=pltpu.VMEM)
+    hbm = pl.BlockSpec(memory_space=pltpu.HBM)
     smem = pl.BlockSpec(memory_space=pltpu.SMEM)
     dma = pltpu.SemaphoreType.DMA
     return pl.pallas_call(
@@ -461,7 +495,7 @@
             jax.ShapeDtypeStruct((pts, hid), BF),
             jax.ShapeDtypeStruct((hid // (4 * NZ), feat), F32),
         ),
-        in_specs=[smem, smem, vmem, vmem, vmem, vmem],
+        in_specs=[smem, smem, hbm, hbm, hbm, hbm],
         out_specs=(vmem, vmem),
         scratch_shapes=[
             pltpu.VMEM((n_rows, hid + AUX), BF),
@@ -475,13 +509,13 @@
             pltpu.VMEM((4, pts, feat), BF),
             pltpu.VMEM((4, pts, feat), BF),
             pltpu.VMEM((hid, feat), F32),
-            pltpu.VMEM((2, 2, NZ, size, feat), BF),
-            pltpu.VMEM((2, 2, NZ // 2, size, feat), BF),
-            pltpu.VMEM((NX, NY, NZ // 2, size, 128), BF),
-            pltpu.VMEM((NZ // 2, size, 128), BF),
-            pltpu.VMEM((NZ, size, 128), BF),
-            pltpu.VMEM((size, 128), F32),
-            pltpu.VMEM((NX, size, 128), F32),
+            pltpu.VMEM((2, 2, 2, 2, 2 * size, feat), BF),
+            pltpu.VMEM((2, 2, 2, 2 * size, feat), BF),
+            pltpu.VMEM((NX, NY, 2, 2 * size, 128), BF),
+            pltpu.VMEM((2, 2 * size, 128), BF),
+            pltpu.VMEM((NZ, 2 * size, 128), BF),
+            pltpu.VMEM((2, size, 128), BF),
+            pltpu.VMEM((NX, size, 128), BF),
             dma((28,)),
             dma((NZ, 4)),
             dma((60,)),
@@ -496,14 +530,18 @@
             dma((NX, NY)),
             dma((NZ,)),
             dma((NZ,)),
-            dma((NX, 2)),
+            dma((NX, 2, 2)),
             dma((NX,)),
+            pltpu.VMEM((hid, feat), BF),
+            pltpu.VMEM((1, pts), BF),
+            pltpu.VMEM((2 * probes, pts), BF),
+            dma((4,)),
         ],
         compiler_params=pltpu.CompilerParams(
-            collective_id=0, has_side_effects=True, vmem_limit_bytes=56 << 20
+            collective_id=0, has_side_effects=True, vmem_limit_bytes=28 << 20
         ),
         name="fused",
-    )(amplitude, length_sq, hidden, projection, alpha[None, :], probe_pairs.T)
+    )(amplitude, length_sq, *(pltpu.with_memory_space_constraint(a, pltpu.HBM) for a in (hidden, projection, alpha[None, :], probe_pairs.T)))
 
 
 def per_device(hidden, projection, alpha, probe_pairs, amplitude, length_sq):

time: 68.9 us -> 66.5 us (0.965)
  Pallas kernels: 64.6 us -> 63.2 us
  local copies, waits for them, and re-layouts: 2.25 us -> 1.3 us
    pallas_call x1, Pallas kernels: 64.6 us -> 63.2 us  [fused(): pl.pallas_call(functools.partial(kernel, probes), out_shape=(jax.ShapeDty...]
    unnamed x4 -> x2, local copies, waits for them, and re-layouts: 2.25 us -> 1.3 us
where the time goes in v4:
time: 66.5 us; the launch traced here: 66.4 us
  Pallas kernels  63.2 us (95%)
  between operations  1.93 us (3%)
  local copies, waits for them, and re-layouts  1.3 us (2%)
    pallas_call x1, Pallas kernels, fused(): pl.pallas_call(functools.partial(kernel, probes), out_shape=(jax.ShapeDty...  63.2 us

profile of v4, /device:TPU:1, one launch (start us, length us, event | category | flops | bytes accessed | tf_op | source)
XLA Modules:
  0.0 66.4 jit_solution(7464649724952894805)
XLA Ops:
  1.9 63.2 %fused.1 = (bf16[128,768]{1,0:T(8,128)(2,1)S(1)}, f32[24,512]{1,0:T(8,128)S(1)}) custom-call(f32[1]{0:T(128)S(6)} %copy.10.amp_ref, f32[1]{0:T(128)S(6)} %copy.11.lsq_ref, bf16[128,768]{1,0:T(8,128)(2,1)} %hidden_hbm.1, bf16[768,512]{1,0:T(8,128)(2,1)} %proj_hbm.1, bf16[1,128]{1,0:T(2,128)(2,1)} %bitcast.3, bf16[32,128]{1,0:T(8,128)(2,1)} %bitcast.2), custom_call_target="tpu_custom_call" | custom-call | tf_op jit(solution)/shard_map/fused/pallas_call | solution.py:492
  65.1 0.7 %copy.12 = bf16[128,768]{1,0:T(8,128)(2,1)} copy(bf16[128,768]{1,0:T(8,128)(2,1)S(1)} %get-tuple-element.4) | data formatting | bytes 393216
  65.8 0.6 copy.13

commit v5 on v4

--- a/solution.py
+++ b/solution.py
@@ -18,7 +18,10 @@
 POS = {0: 0, 4: 1, 3: 2, 5: 3, 2: 4, 6: 5, 1: 6, 7: 7}
 GROUPS = 4
 CHUNK = 1024
+MERGE = 2
+LATE = 0
 PARTS = 4
+ROW_PARTS = 4
 SLOTS = [
     (0, 0, 0), (1, 0, 0), (0, 0, 1), (0, 0, 3), (0, 1, 0), (0, 3, 0), (1, 0, 1), (1, 0, 3),
     (1, 1, 0), (1, 3, 0), (0, 1, 1), (0, 1, 3), (0, 3, 1), (0, 3, 3), (1, 1, 1), (0, 0, 2),
@@ -163,7 +166,7 @@
     pts, hid = hidden_hbm.shape
     feat = proj_ref.shape[1]
     width = feat + AUX
-    half, quarter, piece = pts // 2, pts // 4, pts // PARTS
+    quarter, piece, row_piece = pts // 4, pts // PARTS, pts // ROW_PARTS
     m = 2 * pts
 
     r, c = lax.axis_index("row"), lax.axis_index("col")
@@ -239,7 +242,7 @@
         ).wait_recv()
 
     def row_part(d, q):
-        return rows.at[pl.ds(POS[d] * pts + q * quarter, quarter), :]
+        return rows.at[pl.ds(POS[d] * pts + q * row_piece, row_piece), :]
 
     def col_part(core, dx, dy, q, n):
         start = SLOTS.index((core, dx, dy)) * pts + q * quarter
@@ -282,13 +285,16 @@
             rsum[rs, :] += total
             moved[rs, :] += term
 
-    def finish(g, fresh):
+    def finish(g, fresh, last):
         rs = pl.ds(g * m, m)
         rowsum = jnp.sum(rsum[rs, :], axis=1, keepdims=True)
         value = moved[rs, :] - rowsum * row_feat[rs, :].astype(F32)
         moved[rs, :] = value
         term = lax.dot_general(rows[rs, 0:hid], value.astype(BF), TN, preferred_element_type=F32)
-        terms[...] = term if fresh else terms[...] + term
+        if last:
+            pbuf[...] = ((terms[...] + term) * final).astype(BF).reshape(pbuf.shape)
+        else:
+            terms[...] = term if fresh else terms[...] + term
 
     def pass_on(d, i):
         up = d < 4 or (d == 4 and i < PARTS // 2)
@@ -345,12 +351,12 @@
         elif op[0] == "g":
             g, j = op[1:]
             n = 1
-            while n < 2 and PLAN[at] == ("g", g, j + n):
+            while n < MERGE and PLAN[at] == ("g", g, j + n):
                 at, n = at + 1, n + 1
             chunk(g, j, n, g not in seen)
             seen.add(g)
         elif op[0] == "F":
-            finish(op[1], finished == 0)
+            finish(op[1], finished == 0, finished == GROUPS - 1)
             finished += 1
         elif op[0] == "R":
             pass_on(*op[1:])
@@ -359,7 +365,6 @@
         else:
             col_step(op)
 
-    pbuf[...] = (terms[...] * final).astype(BF).reshape(pbuf.shape)
     send(pbuf.at[:, :, 1 - k], xrec, (pair_send, 0), pair_recv.at[0], partner)
     arrived(xrec, pair_recv.at[0])
     pbuf[:, :, k] = (pbuf[:, :, k].astype(F32) + xrec[...].astype(F32)).astype(BF)
@@ -368,8 +373,8 @@
         lanes = pl.ds(pl.multiple_of(xx * 128, 128), 128)
         return yy // 2, yy % 2, k, slice(None), slice(None), lanes
 
-    for dx in range(NX):
-        for dy in range(NY):
+    for dx in (2, 1, 3, 0):
+        for dy in (2, 1, 3, 0):
             if dx or dy:
                 to = ((NX - dx) % NX, (NY - dy) % NY)
                 send(
@@ -380,16 +385,8 @@
                     dev(dx, dy, 0),
                 )
 
-    for op in PLAN[at:]:
+    for op in PLAN[at : len(PLAN) - LATE]:
         pass_on(*op[1:])
-    for i in range(PARTS):
-        ps = pl.ds(i * piece, piece)
-        arrived(rplus.at[3, ps, :], rs_recv.at[0, 3, i])
-        arrived(rminus.at[3, ps, :], rs_recv.at[1, 3, i])
-    total = moved[0:pts, :] + rplus[3].astype(F32) + rminus[3].astype(F32)
-    grad = (total * final).astype(BF)
-    gh_ref[...] = lax.dot_general(grad, proj_ref[...], NT, preferred_element_type=F32).astype(BF)
-
     share = pbuf[portion(x, y)].astype(F32)
     for dx in range(NX):
         for dy in range(NY):
@@ -430,6 +427,16 @@
             z_recv.at[NZ - dz],
             dev(0, 0, dz),
         )
+
+    for op in PLAN[len(PLAN) - LATE :]:
+        pass_on(*op[1:])
+    for i in range(PARTS):
+        ps = pl.ds(i * piece, piece)
+        arrived(rplus.at[3, ps, :], rs_recv.at[0, 3, i])
+        arrived(rminus.at[3, ps, :], rs_recv.at[1, 3, i])
+    total = moved[0:pts, :] + rplus[3].astype(F32) + rminus[3].astype(F32)
+    grad = (total * final).astype(BF)
+    gh_ref[...] = lax.dot_general(grad, proj_ref[...], NT, preferred_element_type=F32).astype(BF)
 
     @pl.when(gathers)
     def _():
@@ -485,6 +492,7 @@
     width = feat + AUX
     n_rows, n_cols = NZ * pts, 2 * NX * NY * pts
     size = hid // (4 * NZ)
+    arrays = (hidden, projection, alpha[None, :], probe_pairs.T)
     vmem = pl.BlockSpec(memory_space=pltpu.VMEM)
     hbm = pl.BlockSpec(memory_space=pltpu.HBM)
     smem = pl.BlockSpec(memory_space=pltpu.SMEM)
@@ -516,8 +524,8 @@
             pltpu.VMEM((NZ, 2 * size, 128), BF),
             pltpu.VMEM((2, size, 128), BF),
             pltpu.VMEM((NX, size, 128), BF),
-            dma((28,)),
-            dma((NZ, 4)),
+            dma((7 * ROW_PARTS,)),
+            dma((NZ, ROW_PARTS)),
             dma((60,)),
             dma((NX, NY, 4)),
             dma((32,)),
@@ -541,7 +549,7 @@
             collective_id=0, has_side_effects=True, vmem_limit_bytes=28 << 20
         ),
         name="fused",
-    )(amplitude, length_sq, *(pltpu.with_memory_space_constraint(a, pltpu.HBM) for a in (hidden, projection, alpha[None, :], probe_pairs.T)))
+    )(amplitude, length_sq, *(pltpu.with_memory_space_constraint(a, pltpu.HBM) for a in arrays))
 
 
 def per_device(hidden, projection, alpha, probe_pairs, amplitude, length_sq):

time: 66.5 us -> 62.7 us (0.943)
  Pallas kernels: 63.2 us -> 59.4 us
    pallas_call x1, Pallas kernels: 63.2 us -> 59.4 us  [fused(): pl.pallas_call(functools.partial(kernel, probes), out_shape=(jax.ShapeDty...]
where the time goes in v5:
time: 62.7 us; the launch traced here: 62.6 us
  Pallas kernels  59.4 us (95%)
  between operations  1.93 us (3%)
  local copies, waits for them, and re-layouts  1.3 us (2%)
    pallas_call x1, Pallas kernels, fused(): pl.pallas_call(functools.partial(kernel, probes), out_shape=(jax.ShapeDty...  59.4 us
    unnamed x2, local copies, waits for them, and re-layouts  1.3 us

profile of v5, /device:TPU:1, one launch (start us, length us, event | category | flops | bytes accessed | tf_op | source)
XLA Modules:
  0.0 62.6 jit_solution(12527628016550981134)
XLA Ops:
  1.9 59.4 %fused.1 = (bf16[128,768]{1,0:T(8,128)(2,1)S(1)}, f32[24,512]{1,0:T(8,128)S(1)}) custom-call(f32[1]{0:T(128)S(6)} %copy.10.amp_ref, f32[1]{0:T(128)S(6)} %copy.11.lsq_ref, bf16[128,768]{1,0:T(8,128)(2,1)} %hidden_hbm.1, bf16[768,512]{1,0:T(8,128)(2,1)} %proj_hbm.1, bf16[1,128]{1,0:T(2,128)(2,1)} %bitcast.3, bf16[32,128]{1,0:T(8,128)(2,1)} %bitcast.2), custom_call_target="tpu_custom_call" | custom-call | tf_op jit(solution)/shard_map/fused/pallas_call | solution.py:500
  61.3 0.7 %copy.12 = bf16[128,768]{1,0:T(8,128)(2,1)} copy(bf16[128,768]{1,0:T(8,128)(2,1)S(1)} %get-tuple-element.4) | data formatting | bytes 393216
  62.0 0.6 copy.13

commit v6 on v5

--- a/solution.py
+++ b/solution.py
@@ -19,6 +19,7 @@
 GROUPS = 4
 CHUNK = 1024
 MERGE = 2
+EARLY = 4
 LATE = 0
 PARTS = 4
 ROW_PARTS = 4
@@ -366,6 +367,9 @@
             col_step(op)
 
     send(pbuf.at[:, :, 1 - k], xrec, (pair_send, 0), pair_recv.at[0], partner)
+    for op in PLAN[at : at + EARLY]:
+        pass_on(*op[1:])
+    at += EARLY
     arrived(xrec, pair_recv.at[0])
     pbuf[:, :, k] = (pbuf[:, :, k].astype(F32) + xrec[...].astype(F32)).astype(BF)
 

time: 62.7 us -> 62.1 us (level)
  Pallas kernels: 59.4 us -> 58.7 us
    pallas_call x1, Pallas kernels: 59.4 us -> 58.7 us  [fused(): pl.pallas_call(functools.partial(kernel, probes), out_shape=(jax.ShapeDty...]
where the time goes in v6:
time: 62.1 us; the launch traced here: 62 us
  Pallas kernels  58.7 us (95%)
  between operations  1.93 us (3%)
  local copies, waits for them, and re-layouts  1.3 us (2%)
    pallas_call x1, Pallas kernels, fused(): pl.pallas_call(functools.partial(kernel, probes), out_shape=(jax.ShapeDty...  58.7 us
    unnamed x2, local copies, waits for them, and re-layouts  1.3 us

profile of v6, /device:TPU:1, one launch (start us, length us, event | category | flops | bytes accessed | tf_op | source)
XLA Modules:
  0.0 62.0 jit_solution(3931091850139861148)
XLA Ops:
  1.9 58.7 %fused.1 = (bf16[128,768]{1,0:T(8,128)(2,1)S(1)}, f32[24,512]{1,0:T(8,128)S(1)}) custom-call(f32[1]{0:T(128)S(6)} %copy.10.amp_ref, f32[1]{0:T(128)S(6)} %copy.11.lsq_ref, bf16[128,768]{1,0:T(8,128)(2,1)} %hidden_hbm.1, bf16[768,512]{1,0:T(8,128)(2,1)} %proj_hbm.1, bf16[1,128]{1,0:T(2,128)(2,1)} %bitcast.3, bf16[32,128]{1,0:T(8,128)(2,1)} %bitcast.2), custom_call_target="tpu_custom_call" | custom-call | tf_op jit(solution)/shard_map/fused/pallas_call | solution.py:504
  60.7 0.7 %copy.12 = bf16[128,768]{1,0:T(8,128)(2,1)} copy(bf16[128,768]{1,0:T(8,128)(2,1)S(1)} %get-tuple-element.4) | data formatting | bytes 393216
  61.3 0.6 copy.13
